TPU v7x, 32 devices: a whole 2x2x4 slice. The times are simulated.
32 devices in a mesh: pts: 16 (over z, y, x), bev: 2 (over core).
Axes of the slice: x: 2, y: 2, z: 4, core: 2. Of those that a mesh axis runs over, the one named last changes fastest.
Arguments:
- point_feats: float32 [4, 131072], P(None, ('pts', 'bev')), may hold values from -6 to 6
- point_class: int32 [131072], P(('pts', 'bev')), may hold values from 0 to 10
- point_band: int32 [131072], P(('pts', 'bev')), may hold values from 0 to 1
- point_pillar: int32 [131072], P(('pts', 'bev')), may hold values from 0 to 1499
- point_counts: int32 [16], replicated, may hold values from 2048 to 8192
- pillar_cell: int32 [16, 2, 1500], P('pts', 'bev'), may hold values from 0 to 107135, as said below
- class_scores: float32 [11, 11], replicated, may hold values from 0 to 1
- encoder_weight: float32 [64, 15], replicated, may hold values from -1.5 to 1.5
- encoder_bias: float32 [64], replicated, may hold values from -3 to 3
Outputs:
- bev_image: bfloat16 [16, 64, 496, 432], P('pts', None, 'bev')
- class_counts: float32 [11], replicated
Inputs may be any that keep to these rules, and one draw needn't show every extreme that they name: `pillar_cell`: for each frame and band the 1500 cells are distinct.
All inputs are finite; a program needn't handle non-finite values.
Results may differ from a plain program's by a relative error of at most 0.0033.
Values may be sent and summed in bfloat16 or wider, within the bound.
No kernel may reach another device: no remote copies, remote signals or barrier semaphores. Data moves between devices by JAX's collectives and lax.ppermute only.
A program may use at most 128 MiB of HBM per device.

v0:
```python
import jax
import jax.numpy as jnp
from jax import lax
from jax.sharding import PartitionSpec as P

ROWS = 496
COLS = 432
CLASSES = 11
PIL_BAND = 1500


row_block = 256


def encode(raw_values, classes, class_scores, encoder_weight, encoder_bias):
    point_total = classes.shape[0]
    labels = lax.broadcasted_iota(jnp.int32, (class_scores.shape[1], point_total), 0)
    one_hot = (labels == classes[None, :]).astype(jnp.float32)
    painted = jnp.dot(class_scores, one_hot, precision=lax.Precision.HIGHEST)
    inputs = jnp.concatenate([raw_values, painted], axis=0)
    hidden = (
        jnp.dot(encoder_weight, inputs, precision=lax.Precision.HIGHEST) + encoder_bias[:, None]
    )
    return jnp.maximum(hidden, 0.0).astype(jnp.bfloat16)


def pool_pillars(features, segment_ids, column_count, initial):
    point_total = segment_ids.shape[0]
    block_size = min(row_block, point_total)
    block_count = point_total // block_size
    columns = lax.broadcasted_iota(jnp.int32, (block_size, column_count), 1)
    ones_row = jnp.ones((1, point_total), jnp.bfloat16)
    augmented = jnp.concatenate([features, ones_row], axis=0)

    def accumulate(turn_index, pillar_sums):
        row_start = turn_index * block_size
        block_feats = lax.dynamic_slice_in_dim(augmented, row_start, block_size, 1)
        block_ids = lax.dynamic_slice_in_dim(segment_ids, row_start, block_size, 0)
        one_hot = (block_ids[:, None] == columns).astype(jnp.bfloat16)
        return pillar_sums + jnp.dot(block_feats, one_hot, preferred_element_type=jnp.float32)

    return lax.fori_loop(0, block_count, accumulate, initial)


def on_device(
    point_feats,
    point_class,
    point_band,
    point_pillar,
    point_counts,
    pillar_cell,
    class_scores,
    encoder_weight,
    encoder_bias,
):
    band_count = lax.axis_size("bev")
    frame_index = lax.axis_index("pts")
    band_index = lax.axis_index("bev")
    point_total = point_class.shape[0]
    position = band_index * point_total + lax.broadcasted_iota(jnp.int32, (point_total,), 0)
    frame_live = lax.dynamic_index_in_dim(point_counts, frame_index, 0, keepdims=False)
    is_live = position < frame_live
    segment_ids = jnp.where(is_live, point_band * PIL_BAND + point_pillar, band_count * PIL_BAND)
    class_ids = lax.broadcasted_iota(jnp.int32, (CLASSES, 1), 0)
    live_classes = jnp.where(is_live, point_class, CLASSES).reshape(1, -1)
    class_tally = jnp.sum((class_ids == live_classes).astype(jnp.float32), axis=1)
    totals = lax.psum(class_tally, ("pts", "bev"))
    class_counts = totals / point_total
    encoded = encode(point_feats, point_class, class_scores, encoder_weight, encoder_bias)
    channels = encoded.shape[0]
    start = jnp.zeros((channels + 1, band_count * PIL_BAND), jnp.float32)
    partials = pool_pillars(encoded, segment_ids, band_count * PIL_BAND, start)
    owned = lax.psum_scatter(partials, "bev", scatter_dimension=1, tiled=True)
    pillar_mean = (owned[:channels] / jnp.maximum(owned[channels], 1.0)[None, :]).astype(
        jnp.bfloat16
    )
    band_rows = ROWS // band_count
    cell_index = pillar_cell.reshape(-1)
    bev_tile = (
        jnp.zeros((channels, band_rows * COLS), jnp.bfloat16).at[:, cell_index].set(pillar_mean)
    )
    bev_image = bev_tile.reshape(1, channels, band_rows, COLS)
    return (bev_image, class_counts)


def solution(mesh):
    return jax.shard_map(
        on_device,
        mesh=mesh,
        in_specs=(
            P(None, ("pts", "bev")),
            P(("pts", "bev")),
            P(("pts", "bev")),
            P(("pts", "bev")),
            P(),
            P("pts", "bev", None),
            P(),
            P(),
            P(),
        ),
        out_specs=(P("pts", None, "bev", None), P()),
        check_vma=False,
    )
```

profile of v0, /device:TPU:0, one launch (start us, length us, event | category | flops | bytes accessed | tf_op | source)
XLA Modules:
  0.0 146.2 jit_solution(263660152112605280)
XLA Ops:
  7.2 0.0 copy-start
  7.2 0.0 all-reduce.4.cloned.1.call-start
  7.2 1.2 dynamic_slice.18
  8.5 1.0 convolution_bitcast_fusion
  9.5 0.0 copy-done
  9.5 1.9 %fusion.9 = bf16[64,4096]{1,0:T(8,128)(2,1)S(1)} fusion(f32[64,15]{0,1:T(8,128)S(1)} %copy-done, f32[64]{0:T(128)} %param.19, f32[11,4096]{1,0:T(8,128)S(1)} %convolution_bitcast_fusion, f32[4,4096]{1,0:T(4,128)} %param.11), kind=kOutput, calls=%fused_computation.12 | convolution fusion | flops 48033792 | bytes 774144 | tf_op jit(solution)/shard_map/dot_general | solution.py:22
  11.4 1.3 add_select_fusion
  12.7 15.1 %while.14 = (s32[]{:T(128)}, f32[65,3000]{1,0:T(8,128)S(1)}, bf16[65,4096]{1,0:T(8,128)(2,1)S(1)}, s32[4096]{0:T(1024)S(1)}, s32[]{:T(128)}, /*index=5*/s32[]{:T(128)}, s32[]{:T(128)}, s32[]{:T(128)}) while((s32[]{:T(128)}, f32[65,3000]{1,0:T(8,128)S(1)}, bf16[65,4096]{1,0:T(8,128)(2,1)S(1)}, s32[4096]{0:T(1024)S(1)}, s32[]{:T(128)}, ...), condition=%wide.region_1.2_spmd.clone, body=%wide.region_0.1_spmd.clone.sunk | while | flops 100998008 | bytes 1704829 | solution.py:42
  12.7 0.1 dynamic_slice.26
  12.8 0.8 convolution_add_fusion.3
  13.6 0.1 dynamic_slice.26
  13.7 0.8 convolution_add_fusion.3
  14.6 0.1 dynamic_slice.26
  14.6 0.8 convolution_add_fusion.3
  15.5 0.1 dynamic_slice.26
  15.6 0.8 convolution_add_fusion.3
  16.5 0.1 dynamic_slice.26
  16.5 0.8 convolution_add_fusion.3
  17.4 0.1 dynamic_slice.26
  17.5 0.8 convolution_add_fusion.3
  18.3 0.1 dynamic_slice.26
  18.4 0.8 convolution_add_fusion.3
  19.3 0.1 dynamic_slice.26
  19.4 0.8 convolution_add_fusion.3
  20.2 0.1 dynamic_slice.26
  20.3 0.8 convolution_add_fusion.3
  21.2 0.1 dynamic_slice.26
  21.3 0.8 convolution_add_fusion.3
  22.1 0.1 dynamic_slice.26
  22.2 0.8 convolution_add_fusion.3
  23.1 0.1 dynamic_slice.26
  23.1 0.8 convolution_add_fusion.3
  24.0 0.1 dynamic_slice.26
  24.1 0.8 convolution_add_fusion.3
  24.9 0.1 dynamic_slice.26
  25.0 0.8 convolution_add_fusion.3
  25.9 0.1 dynamic_slice.26
  26.0 0.8 convolution_add_fusion.3
  26.8 0.1 dynamic_slice.26
  26.9 0.8 convolution_add_fusion.3
  27.8 0.0 copy-start.1
  27.8 0.9 copy-done.1
  28.7 0.0 all-reduce.4.cloned.1.call-update
  28.7 1.3 fusion.16
  30.0 0.2 convert_reduce_fusion
  30.1 42.0 %psum.7 = f32[11]{0:T(128)S(1)} all-reduce(f32[11]{0:T(128)S(1)} %convert_reduce_fusion), channel_id=1, replica_groups=mesh['pts'=16,'bev'=2] {'pts','bev'}, use_global_device_ids=true, to_apply=%region_5.6 | all-reduce | flops 11 | bytes 88 | tf_op jit(solution)/shard_map/psum | solution.py:67
  72.1 1.2 dynamic-slice
  74.0 0.7 fusion.17
  74.7 0.5 broadcast_multiply_fusion
  75.3 0.0 all-reduce.4.cloned.1.call-done
  75.3 0.9 fusion.18
  76.2 1.2 fusion.14
  77.3 0.3 copy.19
  77.6 21.5 %scatter_custom_fusion = bf16[64,107136]{0,1:T(8,128)(2,1)} fusion(s32[1500]{0:T(1024)S(1)} %fusion.17, bf16[1500,64]{1,0:T(8,128)(2,1)S(1)} %copy.19, bf16[]{:T(256)} %constant.53.clone.1), kind=kCustom, calls=%fused_computation.7 | custom fusion | bytes 13713410 | tf_op jit(solution)/shard_map/scatter | solution.py:80
  99.1 40.2 %copy.20 = bf16[1,64,248,432]{2,3,1,0:T(8,128)(2,1)} copy(bf16[1,64,248,432]{1,3,2,0:T(8,128)(2,1)} %bitcast.16) | data formatting | bytes 27426816
  (2 shorter events, 0.0 us)
Async XLA Ops:
  7.2 2.3 %copy-start = (f32[64,15]{0,1:T(8,128)S(1)}, f32[64,15]{0,1:T(8,128)}, u32[]{:S(2)}) copy-start(f32[64,15]{0,1:T(8,128)} %param.18) | copy-start | bytes 11524
  7.2 68.1 %all-reduce.4.cloned.1.call-start = ((), (), s32[]{:S(2)}) async-start(), calls=%async_computation | async-start | bytes 1769472
  27.8 0.9 copy-start.1
Sparse Core Ops, SparseCore 0:
  28.8 21.8 all-reduce.3
where the time goes:
time: 148 us; the launch traced here: 146 us
  local copies, waits for them, and re-layouts  66.6 us (45%)
  blocking collectives  42 us (28%)
  matrix products  16.2 us (11%)
  between operations  14.8 us (10%)
  other arithmetic  6.05 us (4%)
    unnamed x6, local copies, waits for them, and re-layouts  42.4 us
    psum x1, blocking collectives, on_device(): totals = lax.psum(class_tally, ('pts', 'bev'))  42 us
    scatter x1, local copies, waits for them, and re-layouts, on_device(): jnp.zeros((channels, band_rows * COLS), jnp.bfloat16).at[:, cell_index]  21.5 us
    dot_general x16, matrix products, accumulate(): jnp.dot(block_feats, one_hot, preferred_element_type=jnp.float32)  13.4 us
  transfers between devices with their start and end apart: 1, of which 0 were waited for; matrix products, arithmetic and copies ran while one was open for 3% of the time, Pallas kernels for 0%

commit v1 on v0

v1 whole, which is shorter than its diff:
```python
import jax
import jax.numpy as jnp
from jax import lax
from jax.experimental import pallas as pl
from jax.experimental.pallas import tpu as pltpu
from jax.sharding import PartitionSpec as P

ROWS = 496
COLS = 432
CLASSES = 11

LO = 256
STEP = 16
BUCKETS = 32
HIGHEST = lax.Precision.HIGHEST
NT = (((1,), (1,)), ((), ()))


def round_up(value, unit):
    return -(-value // unit) * unit


def iota(shape, axis):
    return lax.broadcasted_iota(jnp.int32, shape, axis)


def to_f32(mask):
    return jnp.where(mask, 1.0, 0.0).astype(jnp.float32)


def split3(value):
    high = value.astype(jnp.bfloat16).astype(jnp.float32)
    rest = value - high
    mid = rest.astype(jnp.bfloat16).astype(jnp.float32)
    return high, mid, rest - mid


def encoder_matrix(weight, scores, bias_row):
    channels, columns = weight.shape
    lane = iota((columns, 80), 1)
    row = iota((columns, 80), 0)
    pick = to_f32((lane < 24) & ((lane & 3) == row))
    shift = to_f32(iota((columns, CLASSES), 0) == iota((columns, CLASSES), 1) + 4)
    place_lane = iota((CLASSES, 80), 1)
    place = to_f32((place_lane >= 32) & ((place_lane & 15) == iota((CLASSES, 80), 0)))
    spread = jnp.dot(
        jnp.dot(shift, scores, precision=HIGHEST, preferred_element_type=jnp.float32),
        place,
        precision=HIGHEST,
        preferred_element_type=jnp.float32,
    )
    matrix = jnp.dot(
        weight, pick + spread, precision=HIGHEST, preferred_element_type=jnp.float32
    )
    eye = iota((channels, channels), 0) == iota((channels, channels), 1)
    bias = jnp.sum(jnp.where(eye, bias_row, 0.0), axis=1, keepdims=True)
    out_lane = iota((channels, 80), 1)
    matrix = matrix + jnp.where((out_lane >= 32) & ((out_lane & 15) == CLASSES), bias, 0.0)
    high, mid, low = split3(matrix)
    take_mid = ((out_lane >= 8) & (out_lane < 16)) | ((out_lane >= 48) & (out_lane < 64))
    take_low = ((out_lane >= 16) & (out_lane < 20)) | (out_lane >= 64)
    return jnp.where(take_mid, mid, jnp.where(take_low, low, high)).astype(jnp.bfloat16)


def two_level(values, hi, lo, hi_count):
    rows, total = values.shape
    tall = [values * to_f32(hi == h).astype(jnp.bfloat16) for h in range(hi_count)]
    one_hot = to_f32(iota((LO, total), 0) == lo).astype(jnp.bfloat16)
    return tall, one_hot


def pool_body(
    parts, spans, pillars, sub_of, *refs
):
    point_refs = refs[: 4 * parts]
    counts_ref, cell_ref, scores_ref, weight_ref, bias_ref = refs[4 * parts : 4 * parts + 5]
    sorted_ref, starts_ref, tally_ref = refs[4 * parts + 5 : 4 * parts + 8]
    cell_pad = refs[4 * parts + 8]
    frame = lax.axis_index("pts")
    band = lax.axis_index("bev")
    live_total = counts_ref[frame]
    channels = weight_ref.shape[0]
    hi_count = round_up(pillars, LO) // LO
    width = hi_count * LO

    matrix = encoder_matrix(weight_ref[...], scores_ref[...], bias_ref[...])
    sums = jnp.zeros((hi_count * channels + 16, LO), jnp.float32)
    tally = jnp.zeros((16, 1), jnp.float32)
    for part in range(parts):
        feats, classes, bands, pillar = [r[...] for r in point_refs[4 * part : 4 * part + 4]]
        feats = feats.reshape(feats.shape[-2:])
        classes = classes.reshape(1, -1)
        bands = bands.reshape(1, -1)
        pillar = pillar.reshape(1, -1)
        total = feats.shape[1]
        position = spans[part](band) * total + iota((1, total), 1)
        live = position < live_total
        live_class = jnp.where(live, classes, CLASSES)
        one_hot = to_f32(iota((16, total), 0) == live_class)
        tally = tally + jnp.sum(one_hot, axis=1, keepdims=True)
        one_hot = jnp.where(iota((16, total), 0) == CLASSES, 1.0, one_hot)
        high, mid, low = split3(jnp.concatenate([feats, feats], axis=0))
        top = iota((8, total), 0) < 4
        first = jnp.where(top, high, mid)
        third = jnp.where(top, high, low)
        stacked = jnp.concatenate(
            [first, first, third, jnp.zeros_like(first), one_hot, one_hot, one_hot], axis=0
        ).astype(jnp.bfloat16)
        hidden = jnp.dot(matrix, stacked, preferred_element_type=jnp.float32)
        encoded = jnp.maximum(hidden, 0.0).astype(jnp.bfloat16)
        hi = jnp.where(live & (bands == band), pillar >> 8, 15)
        lo = pillar & (LO - 1)
        tall, lo_hot = two_level(encoded, hi, lo, hi_count)
        tall.append(to_f32(iota((16, total), 0) == hi).astype(jnp.bfloat16))
        sums = sums + lax.dot_general(
            jnp.concatenate(tall, axis=0), lo_hot, NT, preferred_element_type=jnp.float32
        )
    diagonal = iota((16, 128), 0) == iota((16, 128), 1)
    tally_ref[...] = jnp.sum(jnp.where(diagonal, tally, 0.0), axis=0, keepdims=True)

    cell_pad[...] = jnp.full(cell_pad.shape, -1, jnp.int32)
    cell_pad[:, :pillars] = cell_ref[...].reshape(1, pillars)
    cell = cell_pad[...]
    cell_f = cell.astype(jnp.float32)
    grid_row = jnp.floor((cell_f + 0.5) * (1.0 / COLS)).astype(jnp.int32)
    grid_col = cell - grid_row * COLS
    sub, lane = (grid_col, grid_row) if sub_of == "col" else (grid_row, grid_col)
    block = jnp.where(cell >= 0, sub >> 4, BUCKETS - 1)
    member = to_f32(iota((BUCKETS, width), 0) == block)
    before = to_f32(iota((LO, LO), 0) < iota((LO, LO), 1)).astype(jnp.bfloat16)
    offset = jnp.zeros((BUCKETS, 1), jnp.float32)
    ranks = []
    for h in range(hi_count):
        chunk = member[:, h * LO : (h + 1) * LO]
        prefix = jnp.dot(
            chunk.astype(jnp.bfloat16), before, preferred_element_type=jnp.float32
        )
        ranks.append(prefix + offset)
        offset = offset + jnp.sum(chunk, axis=1, keepdims=True)
    square = iota((BUCKETS, 128), 0)
    across = iota((BUCKETS, 128), 1)
    starts_row = jnp.sum(jnp.where(square < across, offset, 0.0), axis=0, keepdims=True)
    starts_ref[...] = starts_row.astype(jnp.int32)
    start = jnp.sum(jnp.where(square == across, starts_row, 0.0), axis=1, keepdims=True)
    placed = jnp.zeros((hi_count * (channels + 16), LO), jnp.float32)
    extra = iota((16, LO), 0)
    counts = sums[hi_count * channels :]
    for h in range(hi_count):
        at = slice(h * LO, (h + 1) * LO)
        rank = jnp.sum(member[:, at] * (ranks[h] + start), axis=0, keepdims=True).astype(jnp.int32)
        mean = sums[h * channels : (h + 1) * channels] / jnp.maximum(counts[h : h + 1], 1.0)
        sub_h = sub[:, at]
        lane_h = lane[:, at]
        where = jnp.where(
            extra == 0,
            block[:, at],
            jnp.where(
                extra == 1,
                sub_h & (STEP - 1),
                jnp.where(extra == 2, lane_h >> 8, jnp.where(extra == 3, lane_h & 255, 0)),
            ),
        ).astype(jnp.float32)
        values = jnp.concatenate([mean, where], axis=0).astype(jnp.bfloat16)
        tall, lo_hot = two_level(values, rank >> 8, rank & (LO - 1), hi_count)
        placed = placed + lax.dot_general(
            jnp.concatenate(tall, axis=0), lo_hot, NT, preferred_element_type=jnp.float32
        )
    rows = channels + 16
    tail = iota((8, LO), 0)
    for h in range(hi_count):
        at = slice(h * LO, (h + 1) * LO)
        piece = placed[h * rows : (h + 1) * rows]
        sorted_ref[:channels, at] = piece[:channels]
        sub_s = piece[channels : channels + 1] * STEP + piece[channels + 1 : channels + 2]
        lane_s = piece[channels + 2 : channels + 3] * 256.0 + piece[channels + 3 : channels + 4]
        sorted_ref[channels:, at] = jnp.where(tail == 0, sub_s, jnp.where(tail == 1, lane_s, 0.0))
    sorted_ref[:, width:] = jnp.full((channels + 8, LO), 0.0, jnp.float32)
    sorted_ref[channels:, width:] = jnp.full((8, LO), -1.0, jnp.float32)


def place_body(first_block, starts_ref, sorted_ref, out_ref, acc_ref):
    block = pl.program_id(0) + first_block
    channels, step, lanes = out_ref.shape
    wide = round_up(lanes, 128)
    begin = starts_ref[0, block]
    end = starts_ref[0, block + 1]
    base = (begin >> 7) << 7
    turns = (end - base + LO - 1) // LO

    def partial(turn):
        at = pl.ds(pl.multiple_of(base + turn * LO, 128), LO)
        sub = sorted_ref[channels : channels + 1, at].astype(jnp.int32) - block * step
        lane = sorted_ref[channels + 1 : channels + 2, at].astype(jnp.int32)
        mask = to_f32(iota((step, LO), 0) == sub)
        mean = sorted_ref[:channels, at]
        tall = (mean[:, None, :] * mask[None]).reshape(channels * step, LO).astype(jnp.bfloat16)
        lane_hot = to_f32(iota((wide, LO), 0) == lane).astype(jnp.bfloat16)
        return lax.dot_general(tall, lane_hot, NT, preferred_element_type=jnp.float32)

    def put(value):
        out_ref[...] = value.astype(jnp.bfloat16).reshape(channels, step, wide)[:, :, :lanes]

    @pl.when(turns <= 1)
    def _():
        put(partial(0))

    @pl.when(turns > 1)
    def _():
        acc_ref[...] = partial(0)

        @pl.loop(1, turns)
        def _(turn):
            acc_ref[...] += partial(turn)

        put(acc_ref[...])


def place(sorted_values, starts, channels, subs, lanes):
    wide = round_up(lanes, 128)
    blocks = pl.cdiv(subs, STEP)
    return pl.pallas_call(
        lambda *refs: place_body(0, *refs),
        grid_spec=pltpu.PrefetchScalarGridSpec(
            num_scalar_prefetch=1,
            grid=(blocks,),
            in_specs=[pl.BlockSpec(sorted_values.shape, lambda b, s: (0, 0))],
            out_specs=pl.BlockSpec((channels, STEP, lanes), lambda b, s: (0, b, 0)),
            scratch_shapes=[pltpu.VMEM((channels * STEP, wide), jnp.float32)],
        ),
        out_shape=jax.ShapeDtypeStruct((channels, subs, lanes), jnp.bfloat16),
        compiler_params=pltpu.CompilerParams(dimension_semantics=("arbitrary",)),
        name="place",
    )(starts, sorted_values)


def on_device(
    point_feats,
    point_class,
    point_band,
    point_pillar,
    point_counts,
    pillar_cell,
    class_scores,
    encoder_weight,
    encoder_bias,
):
    band_count = lax.axis_size("bev")
    frames = lax.axis_size("pts")
    total = point_class.shape[0]
    pillars = pillar_cell.shape[-1]
    channels = encoder_weight.shape[0]
    band_rows = ROWS // band_count
    own = (
        point_feats,
        point_class.reshape(1, -1),
        point_band.reshape(1, -1),
        point_pillar.reshape(1, -1),
    )
    if band_count == 2:
        peer = tuple(lax.ppermute(x, "bev", [(0, 1), (1, 0)]) for x in own)
        points = own + peer
        spans = (lambda band: band, lambda band: 1 - band)
    else:
        gathered = [lax.all_gather(x, "bev", axis=0) for x in own]
        points = tuple(x[i] for i in range(band_count) for x in gathered)
        spans = tuple((lambda band, i=i: i) for i in range(band_count))
    parts = len(spans)

    def tiles(subs, lanes):
        return round_up(subs, 16) * round_up(lanes, 128)

    sub_of = "col" if tiles(COLS, band_rows) <= tiles(band_rows, COLS) else "row"
    subs, lanes = (COLS, band_rows) if sub_of == "col" else (band_rows, COLS)
    width = round_up(pillars, LO)
    vmem = pl.BlockSpec(memory_space=pltpu.VMEM)
    smem = pl.BlockSpec(memory_space=pltpu.SMEM)
    sorted_values, starts, tally = pl.pallas_call(
        lambda *refs: pool_body(parts, spans, pillars, sub_of, *refs),
        in_specs=[vmem] * (4 * parts) + [smem] + [vmem] * 4,
        out_specs=(vmem, vmem, vmem),
        out_shape=(
            jax.ShapeDtypeStruct((channels + 8, width + LO), jnp.float32),
            jax.ShapeDtypeStruct((1, 128), jnp.int32),
            jax.ShapeDtypeStruct((1, 128), jnp.float32),
        ),
        scratch_shapes=[pltpu.VMEM((1, width), jnp.int32)],
        name="pool",
    )(
        *points,
        point_counts,
        pillar_cell.reshape(1, pillars),
        class_scores,
        encoder_weight,
        encoder_bias.reshape(1, channels),
    )
    stride = 1
    while stride < frames:
        pairs = [(i, i ^ stride) for i in range(frames)]
        tally = tally + lax.ppermute(tally, "pts", pairs)
        stride *= 2
    class_counts = tally[0, :CLASSES] / total
    planes = place(sorted_values, starts, channels, subs, lanes)
    bev_image = planes.swapaxes(1, 2) if sub_of == "col" else planes
    return (bev_image[None], class_counts)


def solution(mesh):
    return jax.shard_map(
        on_device,
        mesh=mesh,
        in_specs=(
            P(None, ("pts", "bev")),
            P(("pts", "bev")),
            P(("pts", "bev")),
            P(("pts", "bev")),
            P(),
            P("pts", "bev", None),
            P(),
            P(),
            P(),
        ),
        out_specs=(P("pts", None, "bev", None), P()),
        check_vma=False,
    )
```

time: 148 us -> 43.9 us (0.30); the launches traced: 146 us -> 43.6 us
  local copies, waits for them, and re-layouts: 66.6 us -> 2.02 us
  blocking collectives: 42 us -> 0 us
  Pallas kernels: 0 us -> 23.7 us
  matrix products: 16.2 us -> 0 us
  between operations: 14.8 us -> 0.69 us
  starting transfers between devices: 0.04 us -> 11.2 us
  other arithmetic: 6.05 us -> 1.15 us
  waiting for transfers between devices: 0.02 us -> 4.86 us
    psum x1 -> x0, blocking collectives: 42 us -> none  [on_device(): totals = lax.psum(class_tally, ('pts', 'bev'))]
    unnamed x6 -> x9, local copies, waits for them, and re-layouts: 42.4 us -> 2.02 us
    pallas_call x0 -> x2, Pallas kernels: none -> 23.7 us  [the longest x1 17.8 us: place(): pl.pallas_call(lambda *refs: place_body(0, *refs), grid_spec=pltpu.Prefet...]
    scatter x1 -> x0, local copies, waits for them, and re-layouts: 21.5 us -> none  [on_device(): jnp.zeros((channels, band_rows * COLS), jnp.bfloat16).at[:, cell_index]]
    dot_general x18 -> x0, matrix products: 16.2 us -> none  [the longest x16 13.4 us: accumulate(): jnp.dot(block_feats, one_hot, preferred_element_type=jnp.float32)]
    ppermute x0 -> x8, starting transfers between devices: none -> 11.2 us  [the longest x4 10.1 us: on_device(): tally = tally + lax.ppermute(tally, 'pts', pairs)]
    ppermute x0 -> x8, waiting for transfers between devices: none -> 4.86 us  [the longest x4 4.85 us: on_device(): tally = tally + lax.ppermute(tally, 'pts', pairs)]
    select_n x3 -> x0, other arithmetic: 3.3 us -> none  [the longest x1 1.3 us: on_device(): jnp.where(is_live, point_band * PIL_BAND + point_pillar, band_count * PIL...]
  transfers between devices with their start and end apart: 1 -> 8, of which waited for: 0 -> 3; matrix products, arithmetic and copies ran while one was open for 3% -> 3% of each run, Pallas kernels for 0% -> 41%
where the time goes in v1:
time: 43.9 us; the launch traced here: 43.6 us
  Pallas kernels  23.7 us (54%)
  starting transfers between devices  11.2 us (26%)
  waiting for transfers between devices  4.86 us (11%)
  local copies, waits for them, and re-layouts  2.02 us (5%)
  other arithmetic  1.15 us (3%)
  between operations  0.69 us (2%)
    pallas_call x1, Pallas kernels, place(): pl.pallas_call(lambda *refs: place_body(0, *refs), grid_spec=pltpu.Prefet...  17.8 us
    ppermute x4, starting transfers between devices, on_device(): tally = tally + lax.ppermute(tally, 'pts', pairs)  10.1 us
    pallas_call x1, Pallas kernels, on_device(): pl.pallas_call(lambda *refs: pool_body(parts, spans, pillars, sub_of, *re...  5.95 us
    ppermute x4, waiting for transfers between devices, on_device(): tally = tally + lax.ppermute(tally, 'pts', pairs)  4.85 us
    unnamed x9, local copies, waits for them, and re-layouts  2.02 us
    ppermute x4, starting transfers between devices, on_device(): peer = tuple((lax.ppermute(x, 'bev', [(0, 1), (1, 0)]) for x in own))  1.15 us
  transfers between devices with their start and end apart: 8, of which 3 were waited for; matrix products, arithmetic and copies ran while one was open for 3% of the time, Pallas kernels for 41%

profile of v1, /device:TPU:0, one launch (start us, length us, event | category | flops | bytes accessed | tf_op | source)
XLA Modules:
  0.0 43.6 jit_solution(14862754686427687660)
XLA Ops:
  0.6 0.6 %collective-permute-start = (f32[4,4096]{1,0:T(4,128)}, f32[4,4096]{1,0:T(4,128)S(1)}, u32[]{:S(2)}, u32[]{:S(2)}) collective-permute-start(f32[4,4096]{1,0:T(4,128)} %refs_0_.1), channel_id=1, source_target_pairs={{0,1},{1,0},{2,3},{3,2},{4,5},{5,4},{6,7},{7,6},{8,9},{9,8},{10,11... | collective-permute-start | bytes 196616 | tf_op jit(solution)/shard_map/ppermute | solution.py:260
  1.2 0.1 collective-permute-start.1
  1.3 0.4 collective-permute-start.2
  1.7 0.1 collective-permute-start.3
  1.8 1.4 %copy.11.refs_11_ = f32[64,15]{1,0:T(8,128)} copy(f32[64,15]{0,1:T(8,128)} %param.16) | data formatting | bytes 7680 | tf_op args[7]
  3.2 0.0 collective-permute-done.1.refs_5_
  3.2 0.0 copy-start.1
  3.2 0.0 collective-permute-done.2.refs_6_
  3.2 0.0 copy-start.2
  3.2 0.0 collective-permute-done.3.refs_7_
  3.2 0.0 copy-start.3
  3.2 0.0 collective-permute-done.refs_4_
  3.2 0.0 copy-start
  3.2 0.5 %copy-done.1 = s32[1,4096]{1,0:T(1,128)} copy-done((s32[1,4096]{1,0:T(1,128)}, s32[1,4096]{1,0:T(1,128)S(1)}, u32[]{:S(2)}) %copy-start.1) | copy-done | bytes 16408
  3.8 0.0 copy-done.2
  3.8 0.0 copy-done.3
  3.8 0.1 copy-done
  3.9 5.9 %pool.1 = (f32[72,1792]{1,0:T(8,128)}, s32[1,128]{1,0:T(1,128)}, f32[1,128]{1,0:T(1,128)}) custom-call(f32[4,4096]{1,0:T(4,128)} %refs_0_.1, s32[1,4096]{1,0:T(1,128)} %bitcast.12, s32[1,4096]{1,0:T(1,128)} %bitcast.14, s32[1,4096]{1,0:T(1,128)} %bitcast.16, f32[4,4096]{1,0:T(4,128)} %copy-done, s32[1,4096]{1,0:T(1,128)} %copy-done.1, s32[1,4096]{1,0:T(1,128)} %copy-done.2, ...), custom_call_target="tpu_custom_call" | custom-call | tf_op jit(solution)/shard_map/pool/pallas_call | solution.py:277
  9.8 2.9 %collective-permute-start.4 = (f32[1,128]{1,0:T(1,128)}, f32[1,128]{1,0:T(1,128)S(1)}, u32[]{:S(2)}, u32[]{:S(2)}) collective-permute-start(f32[1,128]{1,0:T(1,128)} %get-tuple-element.7), channel_id=1, source_target_pairs={{0,2},{2,0},{4,6},{6,4},{8,10},{10,8},{12,14},{14,12},{16,18},{18,... | collective-permute-start | bytes 1544 | tf_op jit(solution)/shard_map/ppermute | solution.py:299
  12.7 1.8 %collective-permute-done.4 = f32[1,128]{1,0:T(1,128)S(1)} collective-permute-done((f32[1,128]{1,0:T(1,128)}, f32[1,128]{1,0:T(1,128)S(1)}, u32[]{:S(2)}, u32[]{:S(2)}) %collective-permute-start.4) | collective-permute-done | bytes 544 | tf_op jit(solution)/shard_map/ppermute | solution.py:299
  14.5 0.6 %add.12 = f32[1,128]{1,0:T(1,128)S(1)} add(f32[1,128]{1,0:T(1,128)} %get-tuple-element.7, f32[1,128]{1,0:T(1,128)S(1)} %collective-permute-done.4) | non-fusion elementwise | flops 128 | bytes 1536 | tf_op jit(solution)/shard_map/add | solution.py:299
  15.1 2.0 %collective-permute-start.5 = (f32[1,128]{1,0:T(1,128)S(1)}, f32[1,128]{1,0:T(1,128)S(1)}, u32[]{:S(2)}, u32[]{:S(2)}) collective-permute-start(f32[1,128]{1,0:T(1,128)S(1)} %add.12), channel_id=1, source_target_pairs={{0,4},{2,6},{4,0},{6,2},{8,12},{10,14},{12,8},{14,10},{16,20},{18,... | collective-permute-start | bytes 1544 | tf_op jit(solution)/shard_map/ppermute | solution.py:299
  17.1 1.5 %collective-permute-done.5 = f32[1,128]{1,0:T(1,128)S(1)} collective-permute-done((f32[1,128]{1,0:T(1,128)S(1)}, f32[1,128]{1,0:T(1,128)S(1)}, u32[]{:S(2)}, u32[]{:S(2)}) %collective-permute-start.5) | collective-permute-done | bytes 544 | tf_op jit(solution)/shard_map/ppermute | solution.py:299
  18.7 2.1 %collective-permute-start.6 = (f32[1,128]{1,0:T(1,128)S(1)}, f32[1,128]{1,0:T(1,128)S(1)}, u32[]{:S(2)}, u32[]{:S(2)}) collective-permute-start(f32[1,128]{1,0:T(1,128)S(1)} %add.13), channel_id=1, source_target_pairs={{0,8},{2,10},{4,12},{6,14},{8,0},{10,2},{12,4},{14,6},{16,24},{18,... | collective-permute-start | bytes 1544 | tf_op jit(solution)/shard_map/ppermute | solution.py:299
  20.8 1.5 %collective-permute-done.6 = f32[1,128]{1,0:T(1,128)S(1)} collective-permute-done((f32[1,128]{1,0:T(1,128)S(1)}, f32[1,128]{1,0:T(1,128)S(1)}, u32[]{:S(2)}, u32[]{:S(2)}) %collective-permute-start.6) | collective-permute-done | bytes 544 | tf_op jit(solution)/shard_map/ppermute | solution.py:299
  22.3 3.0 %collective-permute-start.7 = (f32[1,128]{1,0:T(1,128)S(1)}, f32[1,128]{1,0:T(1,128)S(1)}, u32[]{:S(2)}, u32[]{:S(2)}) collective-permute-start(f32[1,128]{1,0:T(1,128)S(1)} %add.14), channel_id=1, source_target_pairs={{0,16},{2,18},{4,20},{6,22},{8,24},{10,26},{12,28},{14,30},{16,0},... | collective-permute-start | bytes 1544 | tf_op jit(solution)/shard_map/ppermute | solution.py:299
  25.4 17.8 %place.1 = bf16[64,432,248]{2,1,0:T(8,128)(2,1)} custom-call(s32[1,128]{1,0:T(1,128)} %get-tuple-element.5.refs_0_, f32[72,1792]{1,0:T(8,128)} %get-tuple-element.6.refs_1_), custom_call_target="tpu_custom_call" | custom-call | tf_op jit(solution)/shard_map/place/pallas_call | solution.py:221
  43.1 0.0 collective-permute-done.7
  43.1 0.5 %multiply_bitcast_fusion = f32[11]{0:T(128)} fusion(f32[1,128]{1,0:T(1,128)S(1)} %add.15), kind=kLoop, calls=%fused_computation | loop fusion | flops 11 | bytes 88 | tf_op jit(solution)/shard_map/div | solution.py:301
  (3 shorter events, 0.0 us)
Async XLA Ops:
  0.6 2.6 %collective-permute-start = (f32[4,4096]{1,0:T(4,128)}, f32[4,4096]{1,0:T(4,128)S(1)}, u32[]{:S(2)}, u32[]{:S(2)}) collective-permute-start(f32[4,4096]{1,0:T(4,128)} %refs_0_.1), channel_id=1, source_target_pairs={{0,1},{1,0},{2,3},{3,2},{4,5},{5,4},{6,7},{7,6},{8,9},{9,8},{10,11... | collective-permute-start | bytes 196616 | tf_op jit(solution)/shard_map/ppermute | solution.py:260
  1.2 2.0 %collective-permute-start.1 = (s32[1,4096]{1,0:T(1,128)}, s32[1,4096]{1,0:T(1,128)S(1)}, u32[]{:S(2)}, u32[]{:S(2)}) collective-permute-start(s32[1,4096]{1,0:T(1,128)} %bitcast.11), channel_id=1, source_target_pairs={{0,1},{1,0},{2,3},{3,2},{4,5},{5,4},{6,7},{7,6},{8,9},{9,8},{10,11... | collective-permute-start | bytes 49160 | tf_op jit(solution)/shard_map/ppermute | solution.py:260
  1.3 1.9 %collective-permute-start.2 = (s32[1,4096]{1,0:T(1,128)}, s32[1,4096]{1,0:T(1,128)S(1)}, u32[]{:S(2)}, u32[]{:S(2)}) collective-permute-start(s32[1,4096]{1,0:T(1,128)} %bitcast.13), channel_id=1, source_target_pairs={{0,1},{1,0},{2,3},{3,2},{4,5},{5,4},{6,7},{7,6},{8,9},{9,8},{10,11... | collective-permute-start | bytes 49160 | tf_op jit(solution)/shard_map/ppermute | solution.py:260
  1.7 1.5 %collective-permute-start.3 = (s32[1,4096]{1,0:T(1,128)}, s32[1,4096]{1,0:T(1,128)S(1)}, u32[]{:S(2)}, u32[]{:S(2)}) collective-permute-start(s32[1,4096]{1,0:T(1,128)} %bitcast.15), channel_id=1, source_target_pairs={{0,1},{1,0},{2,3},{3,2},{4,5},{5,4},{6,7},{7,6},{8,9},{9,8},{10,11... | collective-permute-start | bytes 49160 | tf_op jit(solution)/shard_map/ppermute | solution.py:260
  3.2 0.6 %copy-start.1 = (s32[1,4096]{1,0:T(1,128)}, s32[1,4096]{1,0:T(1,128)S(1)}, u32[]{:S(2)}) copy-start(s32[1,4096]{1,0:T(1,128)S(1)} %collective-permute-done.1.refs_5_) | copy-start | bytes 49156
  3.2 0.6 %copy-start.2 = (s32[1,4096]{1,0:T(1,128)}, s32[1,4096]{1,0:T(1,128)S(1)}, u32[]{:S(2)}) copy-start(s32[1,4096]{1,0:T(1,128)S(1)} %collective-permute-done.2.refs_6_) | copy-start | bytes 49156
  3.2 0.6 %copy-start.3 = (s32[1,4096]{1,0:T(1,128)}, s32[1,4096]{1,0:T(1,128)S(1)}, u32[]{:S(2)}) copy-start(s32[1,4096]{1,0:T(1,128)S(1)} %collective-permute-done.3.refs_7_) | copy-start | bytes 49156
  3.2 0.6 %copy-start = (f32[4,4096]{1,0:T(4,128)}, f32[4,4096]{1,0:T(4,128)S(1)}, u32[]{:S(2)}) copy-start(f32[4,4096]{1,0:T(4,128)S(1)} %collective-permute-done.refs_4_) | copy-start | bytes 196612
  9.8 4.7 %collective-permute-start.4 = (f32[1,128]{1,0:T(1,128)}, f32[1,128]{1,0:T(1,128)S(1)}, u32[]{:S(2)}, u32[]{:S(2)}) collective-permute-start(f32[1,128]{1,0:T(1,128)} %get-tuple-element.7), channel_id=1, source_target_pairs={{0,2},{2,0},{4,6},{6,4},{8,10},{10,8},{12,14},{14,12},{16,18},{18,... | collective-permute-start | bytes 1544 | tf_op jit(solution)/shard_map/ppermute | solution.py:299
  15.1 3.6 %collective-permute-start.5 = (f32[1,128]{1,0:T(1,128)S(1)}, f32[1,128]{1,0:T(1,128)S(1)}, u32[]{:S(2)}, u32[]{:S(2)}) collective-permute-start(f32[1,128]{1,0:T(1,128)S(1)} %add.12), channel_id=1, source_target_pairs={{0,4},{2,6},{4,0},{6,2},{8,12},{10,14},{12,8},{14,10},{16,20},{18,... | collective-permute-start | bytes 1544 | tf_op jit(solution)/shard_map/ppermute | solution.py:299
  18.7 3.6 %collective-permute-start.6 = (f32[1,128]{1,0:T(1,128)S(1)}, f32[1,128]{1,0:T(1,128)S(1)}, u32[]{:S(2)}, u32[]{:S(2)}) collective-permute-start(f32[1,128]{1,0:T(1,128)S(1)} %add.13), channel_id=1, source_target_pairs={{0,8},{2,10},{4,12},{6,14},{8,0},{10,2},{12,4},{14,6},{16,24},{18,... | collective-permute-start | bytes 1544 | tf_op jit(solution)/shard_map/ppermute | solution.py:299
  22.3 20.8 %collective-permute-start.7 = (f32[1,128]{1,0:T(1,128)S(1)}, f32[1,128]{1,0:T(1,128)S(1)}, u32[]{:S(2)}, u32[]{:S(2)}) collective-permute-start(f32[1,128]{1,0:T(1,128)S(1)} %add.14), channel_id=1, source_target_pairs={{0,16},{2,18},{4,20},{6,22},{8,24},{10,26},{12,28},{14,30},{16,0},... | collective-permute-start | bytes 1544 | tf_op jit(solution)/shard_map/ppermute | solution.py:299

commit v2 on v1

v2 whole, which is shorter than its diff:
```python
import jax
import jax.numpy as jnp
from jax import lax
from jax.experimental import pallas as pl
from jax.experimental.pallas import tpu as pltpu
from jax.sharding import PartitionSpec as P

ROWS = 496
COLS = 432
CLASSES = 11

LO = 256
STEP = 16
BUCKETS = 32
GROUP = 3
LEADER_ONLY = False
HIGHEST = lax.Precision.HIGHEST
NT = (((1,), (1,)), ((), ()))


def round_up(value, unit):
    return -(-value // unit) * unit


def iota(shape, axis):
    return lax.broadcasted_iota(jnp.int32, shape, axis)


def to_f32(mask):
    return jnp.where(mask, 1.0, 0.0).astype(jnp.float32)


def split3(value):
    high = value.astype(jnp.bfloat16).astype(jnp.float32)
    rest = value - high
    mid = rest.astype(jnp.bfloat16).astype(jnp.float32)
    return high, mid, rest - mid


def encoder_matrix(weight_t, scores, bias_row):
    columns, channels = weight_t.shape
    lane = iota((columns, 80), 1)
    row = iota((columns, 80), 0)
    pick = to_f32((lane < 24) & ((lane & 3) == row))
    shift = to_f32(iota((columns, CLASSES), 0) == iota((columns, CLASSES), 1) + 4)
    place_lane = iota((CLASSES, 80), 1)
    place = to_f32((place_lane >= 32) & ((place_lane & 15) == iota((CLASSES, 80), 0)))
    spread = jnp.dot(
        jnp.dot(shift, scores, precision=HIGHEST, preferred_element_type=jnp.float32),
        place,
        precision=HIGHEST,
        preferred_element_type=jnp.float32,
    )
    matrix = lax.dot_general(
        weight_t,
        pick + spread,
        (((0,), (0,)), ((), ())),
        precision=HIGHEST,
        preferred_element_type=jnp.float32,
    )
    eye = iota((channels, channels), 0) == iota((channels, channels), 1)
    bias = jnp.sum(jnp.where(eye, bias_row, 0.0), axis=1, keepdims=True)
    out_lane = iota((channels, 80), 1)
    matrix = matrix + jnp.where((out_lane >= 32) & ((out_lane & 15) == CLASSES), bias, 0.0)
    high, mid, low = split3(matrix)
    take_mid = ((out_lane >= 8) & (out_lane < 16)) | ((out_lane >= 48) & (out_lane < 64))
    take_low = ((out_lane >= 16) & (out_lane < 20)) | (out_lane >= 64)
    return jnp.where(take_mid, mid, jnp.where(take_low, low, high)).astype(jnp.bfloat16)


def two_level(values, hi, lo, hi_count):
    _, total = values.shape
    tall = [values * to_f32(hi == h).astype(jnp.bfloat16) for h in range(hi_count)]
    one_hot = to_f32(iota((LO, total), 0) == lo).astype(jnp.bfloat16)
    return tall, one_hot


def tally_body(live_of, counts_ref, class_ref, tally_ref):
    classes = class_ref[...]
    live = live_of(counts_ref, classes.shape[1])
    total = classes.shape[1]
    one_hot = to_f32((iota((16, total), 0) == classes) & live)
    tally = jnp.sum(one_hot, axis=1, keepdims=True)
    diagonal = iota((16, 128), 0) == iota((16, 128), 1)
    tally_ref[...] = jnp.sum(jnp.where(diagonal, tally, 0.0), axis=0, keepdims=True)


def live_points(span, counts_ref, total):
    live_total = counts_ref[lax.axis_index("pts")]
    return span(lax.axis_index("bev")) * total + iota((1, total), 1) < live_total


def pool_part(span, hi_count, matrix, counts_ref, feats_ref, class_ref, band_ref, pillar_ref):
    feats = feats_ref[...]
    total = feats.shape[1]
    live = live_points(span, counts_ref, total)
    one_hot = to_f32(iota((16, total), 0) == class_ref[...])
    one_hot = jnp.where(iota((16, total), 0) == CLASSES, 1.0, one_hot)
    high, mid, low = split3(jnp.concatenate([feats, feats], axis=0))
    top = iota((8, total), 0) < 4
    first = jnp.where(top, high, mid)
    third = jnp.where(top, high, low)
    stacked = jnp.concatenate(
        [first, first, third, jnp.zeros_like(first), one_hot, one_hot, one_hot], axis=0
    ).astype(jnp.bfloat16)
    hidden = jnp.dot(matrix, stacked, preferred_element_type=jnp.float32)
    encoded = jnp.maximum(hidden, 0.0).astype(jnp.bfloat16)
    pillar = pillar_ref[...]
    hi = jnp.where(live & (band_ref[...] == lax.axis_index("bev")), pillar >> 8, 15)
    lo = pillar & (LO - 1)
    tall, lo_hot = two_level(encoded, hi, lo, hi_count)
    tall.append(to_f32(iota((16, total), 0) == hi).astype(jnp.bfloat16))
    return lax.dot_general(
        jnp.concatenate(tall, axis=0), lo_hot, NT, preferred_element_type=jnp.float32
    )


def first_body(span, pillars, counts_ref, scores_ref, weight_ref, bias_ref, *refs):
    hi_count = round_up(pillars, LO) // LO
    sums_ref, matrix_ref = refs[4:]
    matrix = encoder_matrix(weight_ref[...], scores_ref[...], bias_ref[...])
    matrix_ref[...] = matrix
    sums_ref[...] = pool_part(span, hi_count, matrix, counts_ref, *refs[:4])


def second_body(spans, pillars, sub_of, counts_ref, matrix_ref, sums_in_ref, cell_ref, *refs):
    parts = len(spans)
    sorted_ref, starts_ref, cell_pad = refs[4 * parts :]
    channels = matrix_ref.shape[0]
    hi_count = round_up(pillars, LO) // LO
    width = hi_count * LO
    sums = sums_in_ref[...]
    for part in range(parts):
        sums = sums + pool_part(
            spans[part], hi_count, matrix_ref[...], counts_ref, *refs[4 * part : 4 * part + 4]
        )

    cell_pad[...] = jnp.full(cell_pad.shape, -1, jnp.int32)
    cell_pad[:, :pillars] = cell_ref[...].reshape(1, pillars)
    cell = cell_pad[...]
    cell_f = cell.astype(jnp.float32)
    grid_row = jnp.floor((cell_f + 0.5) * (1.0 / COLS)).astype(jnp.int32)
    grid_col = cell - grid_row * COLS
    sub, lane = (grid_col, grid_row) if sub_of == "col" else (grid_row, grid_col)
    block = jnp.where(cell >= 0, sub >> 4, BUCKETS - 1)
    member = to_f32(iota((BUCKETS, width), 0) == block)
    before = to_f32(iota((LO, LO), 0) < iota((LO, LO), 1)).astype(jnp.bfloat16)
    offset = jnp.zeros((BUCKETS, 1), jnp.float32)
    ranks = []
    for h in range(hi_count):
        chunk = member[:, h * LO : (h + 1) * LO]
        prefix = jnp.dot(
            chunk.astype(jnp.bfloat16), before, preferred_element_type=jnp.float32
        )
        ranks.append(prefix + offset)
        offset = offset + jnp.sum(chunk, axis=1, keepdims=True)
    square = iota((BUCKETS, 128), 0)
    across = iota((BUCKETS, 128), 1)
    starts_row = jnp.sum(jnp.where(square < across, offset, 0.0), axis=0, keepdims=True)
    size_row = jnp.sum(jnp.where(square == across, offset, 0.0), axis=0, keepdims=True)
    starts_i = starts_row.astype(jnp.int32)
    reach = (starts_i & 127) + size_row.astype(jnp.int32)
    real = iota((1, 128), 1) < BUCKETS - 1
    wide = jnp.max(jnp.where(real, reach, 0), axis=1, keepdims=True) > LO
    starts_ref[...] = jnp.where(iota((1, 128), 1) == 127, wide.astype(jnp.int32), starts_i)
    start = jnp.sum(jnp.where(square == across, starts_row, 0.0), axis=1, keepdims=True)
    placed = jnp.zeros((hi_count * (channels + 16), LO), jnp.float32)
    extra = iota((16, LO), 0)
    counts = sums[hi_count * channels :]
    for h in range(hi_count):
        at = slice(h * LO, (h + 1) * LO)
        rank = jnp.sum(member[:, at] * (ranks[h] + start), axis=0, keepdims=True).astype(jnp.int32)
        mean = sums[h * channels : (h + 1) * channels] / jnp.maximum(counts[h : h + 1], 1.0)
        sub_h = sub[:, at]
        lane_h = lane[:, at]
        where = jnp.where(
            extra == 0,
            block[:, at],
            jnp.where(
                extra == 1,
                sub_h & (STEP - 1),
                jnp.where(extra == 2, lane_h >> 8, jnp.where(extra == 3, lane_h & 255, 0)),
            ),
        ).astype(jnp.float32)
        values = jnp.concatenate([mean, where], axis=0).astype(jnp.bfloat16)
        tall, lo_hot = two_level(values, rank >> 8, rank & (LO - 1), hi_count)
        placed = placed + lax.dot_general(
            jnp.concatenate(tall, axis=0), lo_hot, NT, preferred_element_type=jnp.float32
        )
    rows = channels + 16
    tail = iota((8, LO), 0)
    for h in range(hi_count):
        piece = placed[h * rows : (h + 1) * rows]
        sub_s = piece[channels : channels + 1] * STEP + piece[channels + 1 : channels + 2]
        lane_s = piece[channels + 2 : channels + 3] * 256.0 + piece[channels + 3 : channels + 4]
        extra_s = jnp.where(tail == 0, sub_s, jnp.where(tail == 1, lane_s, 0.0))
        for half in range(2):
            at = slice(half * 128, half * 128 + 128)
            sorted_ref[2 * h + half, :channels, :] = piece[:channels, at]
            sorted_ref[2 * h + half, channels:, :] = extra_s[:, at]
    for chunk in range(2 * hi_count, 2 * hi_count + 2):
        sorted_ref[chunk, :channels, :] = jnp.zeros((channels, 128), jnp.float32)
        sorted_ref[chunk, channels:, :] = jnp.full((8, 128), -1.0, jnp.float32)


def place_body(starts_ref, sorted_ref, out_ref, image, lane_hot, acc_ref, sems):
    channels, _, lanes = out_ref.shape
    chunks, wide, _ = lane_hot.shape
    blocks = image.shape[1] // STEP
    for chunk in range(chunks):
        lane = sorted_ref[chunk, channels + 1 : channels + 2, :].astype(jnp.int32)
        lane_hot[chunk] = to_f32(iota((wide, 128), 0) == lane).astype(jnp.bfloat16)

    def base_of(block):
        return starts_ref[0, block] >> 7

    def partial(block, turn):
        talls = []
        hots = []
        for half in range(2):
            chunk = base_of(block) + 2 * turn + half
            sub = sorted_ref[chunk, channels : channels + 1, :].astype(jnp.int32) - block * STEP
            mask_a = to_f32(iota((8, 128), 0) == sub)
            mask_b = to_f32(iota((8, 128), 0) + 8 == sub)
            tall = []
            for channel in range(channels):
                row = sorted_ref[chunk, pl.ds(channel, 8, stride=0), :]
                tall.append(
                    jnp.concatenate([row * mask_a, row * mask_b], axis=0).astype(jnp.bfloat16)
                )
            talls.append(jnp.concatenate(tall, axis=0))
            hots.append(lane_hot[chunk])
        return lax.dot_general(
            jnp.concatenate(talls, axis=1),
            jnp.concatenate(hots, axis=1),
            NT,
            preferred_element_type=jnp.float32,
        )

    def put(block, value):
        rows = pl.ds(block * STEP, STEP)
        tile = value.astype(jnp.bfloat16).reshape(channels, STEP, wide)
        image[:, rows, :] = tile[:, :, :lanes]

    spans = []
    for begin in range(0, blocks, GROUP):
        spans.append((begin, min(begin + GROUP, blocks)))
    copies = []
    for index, (begin, end) in enumerate(spans):
        rows = pl.ds(begin * STEP, (end - begin) * STEP)
        copies.append(
            pltpu.make_async_copy(image.at[:, rows], out_ref.at[:, rows], sems.at[index])
        )
    spread = starts_ref[0, 127]

    @pl.when(spread == 0)
    def _():
        for (begin, end), copy in zip(spans, copies):
            for block in range(begin, end):
                put(block, partial(block, 0))
            copy.start()

    @pl.when(spread != 0)
    def _():
        @pl.loop(0, blocks)
        def _(block):
            turns = (starts_ref[0, block + 1] - base_of(block) * 128 + LO - 1) // LO
            acc_ref[...] = partial(block, 0)

            @pl.loop(1, turns)
            def _(turn):
                acc_ref[...] += partial(block, turn)

            put(pl.multiple_of(block, 1), acc_ref[...])

        for copy in copies:
            copy.start()

    for copy in copies:
        copy.wait()


def place(sorted_values, starts, channels, subs, lanes):
    wide = round_up(lanes, 128)
    blocks = pl.cdiv(subs, STEP)
    groups = pl.cdiv(blocks, GROUP)
    return pl.pallas_call(
        place_body,
        in_specs=[
            pl.BlockSpec(memory_space=pltpu.SMEM),
            pl.BlockSpec(memory_space=pltpu.VMEM),
        ],
        out_specs=pl.BlockSpec(memory_space=pl.ANY),
        scratch_shapes=[
            pltpu.VMEM((channels, blocks * STEP, lanes), jnp.bfloat16),
            pltpu.VMEM((sorted_values.shape[0], wide, 128), jnp.bfloat16),
            pltpu.VMEM((channels * STEP, wide), jnp.float32),
            pltpu.SemaphoreType.DMA((groups,)),
        ],
        out_shape=jax.ShapeDtypeStruct((channels, blocks * STEP, lanes), jnp.bfloat16),
        cost_estimate=pl.CostEstimate(flops=10**9, transcendentals=0, bytes_accessed=10**7),
        name="place",
    )(starts, sorted_values)[:, :subs]


def all_tallies(tally, frames, band_count):
    both = ("pts", "bev")
    leader = band_count - 1
    total = tally
    for shift in range(1, band_count):
        pairs = [((i + shift) % band_count, i) for i in range(band_count)]
        total = total + lax.ppermute(tally, "bev", pairs)
    stride = 1
    while stride < frames:
        radix = 4 if frames % (stride * 4) == 0 else 2
        received = []
        for hop in range(1, radix):
            pairs = []
            for i in range(frames):
                j = i ^ (hop * stride)
                if LEADER_ONLY:
                    pairs.append((i * band_count + leader, j * band_count + leader))
                else:
                    pairs.extend((i * band_count + k, j * band_count + k) for k in range(band_count))
            received.append(lax.ppermute(total, both, pairs))
        total = total + sum(received)
        stride *= radix
    if LEADER_ONLY:
        given = [
            lax.ppermute(total, "bev", [(leader, k)])
            for k in range(band_count)
            if k != leader
        ]
        total = jnp.where(lax.axis_index("bev") == leader, total, sum(given))
    return total


def on_device(
    point_feats,
    point_class,
    point_band,
    point_pillar,
    point_counts,
    pillar_cell,
    class_scores,
    encoder_weight,
    encoder_bias,
):
    band_count = lax.axis_size("bev")
    frames = lax.axis_size("pts")
    total = point_class.shape[0]
    pillars = pillar_cell.shape[-1]
    channels = encoder_weight.shape[0]
    band_rows = ROWS // band_count
    own = (
        point_feats,
        point_class.reshape(1, -1),
        point_band.reshape(1, -1),
        point_pillar.reshape(1, -1),
    )
    others = []
    for shift in range(1, band_count):
        pairs = [((i + shift) % band_count, i) for i in range(band_count)]
        others.extend(lax.ppermute(x, "bev", pairs) for x in own)
    spans = [lambda band, k=k: (band + k) % band_count for k in range(1, band_count)]

    def own_span(band):
        return band

    def tiles(subs, lanes):
        return round_up(subs, 16) * round_up(lanes, 128)

    sub_of = "col" if tiles(COLS, band_rows) <= tiles(band_rows, COLS) else "row"
    subs, lanes = (COLS, band_rows) if sub_of == "col" else (band_rows, COLS)
    width = round_up(pillars, LO)
    vmem = pl.BlockSpec(memory_space=pltpu.VMEM)
    smem = pl.BlockSpec(memory_space=pltpu.SMEM)
    tally = pl.pallas_call(
        lambda *refs: tally_body(lambda c, t: live_points(own_span, c, t), *refs),
        in_specs=[smem, vmem],
        out_specs=vmem,
        out_shape=jax.ShapeDtypeStruct((1, 128), jnp.float32),
        name="tally",
    )(point_counts, own[1])
    class_counts = (all_tallies(tally, frames, band_count) / total)[0, :CLASSES]
    hi_count = width // LO
    sums, matrix = pl.pallas_call(
        lambda *refs: first_body(own_span, pillars, *refs),
        in_specs=[smem] + [vmem] * 7,
        out_specs=(vmem, vmem),
        out_shape=(
            jax.ShapeDtypeStruct((hi_count * channels + 16, LO), jnp.float32),
            jax.ShapeDtypeStruct((channels, 80), jnp.bfloat16),
        ),
        cost_estimate=pl.CostEstimate(flops=10**9, transcendentals=0, bytes_accessed=10**6),
        name="pool_own",
    )(
        point_counts,
        class_scores,
        encoder_weight.T,
        encoder_bias.reshape(1, channels),
        *own,
    )
    sorted_values, starts = pl.pallas_call(
        lambda *refs: second_body(spans, pillars, sub_of, *refs),
        in_specs=[smem] + [vmem] * (3 + len(others)),
        out_specs=(vmem, vmem),
        out_shape=(
            jax.ShapeDtypeStruct(((width + LO) // 128, channels + 8, 128), jnp.float32),
            jax.ShapeDtypeStruct((1, 128), jnp.int32),
        ),
        scratch_shapes=[pltpu.VMEM((1, width), jnp.int32)],
        cost_estimate=pl.CostEstimate(flops=10**9, transcendentals=0, bytes_accessed=10**6),
        name="pool_rest",
    )(point_counts, matrix, sums, pillar_cell.reshape(1, pillars), *others)
    planes = place(sorted_values, starts, channels, subs, lanes)
    bev_image = planes.swapaxes(1, 2) if sub_of == "col" else planes
    return (bev_image[None], class_counts)


def solution(mesh):
    return jax.shard_map(
        on_device,
        mesh=mesh,
        in_specs=(
            P(None, ("pts", "bev")),
            P(("pts", "bev")),
            P(("pts", "bev")),
            P(("pts", "bev")),
            P(),
            P("pts", "bev", None),
            P(),
            P(),
            P(),
        ),
        out_specs=(P("pts", None, "bev", None), P()),
        check_vma=False,
    )
```

time: 43.9 us -> 33.8 us (0.77)
  Pallas kernels: 23.7 us -> 16.2 us
  starting transfers between devices: 11.2 us -> 10.2 us
  local copies, waits for them, and re-layouts: 2.02 us -> 1.16 us
  other arithmetic: 1.15 us -> 0.67 us
    pallas_call x2 -> x4, Pallas kernels: 23.7 us -> 16.2 us  [the longest x1 7 us: place(): pl.pallas_call(place_body, in_specs=[pl.BlockSpec(memory_space=pltpu.SMEM...]
    unnamed x9 -> x8, local copies, waits for them, and re-layouts: 2.02 us -> 0.65 us
    ppermute x8 -> x11, starting transfers between devices: 11.2 us -> 10.2 us  [the longest x6 8.73 us: all_tallies(): received.append(lax.ppermute(total, both, pairs))]
    squeeze x0 -> x1, local copies, waits for them, and re-layouts: none -> 0.51 us  [on_device(): class_counts = (all_tallies(tally, frames, band_count) / total)[0, :CLASSES]]
    div x1, other arithmetic: 0.52 us -> 0.01 us  [on_device(): class_counts = (all_tallies(tally, frames, band_count) / total)[0, :CLASSES]]
    ppermute x8 -> x11, waiting for transfers between devices: 4.86 us -> 4.51 us  [the longest x6 3.03 us: all_tallies(): received.append(lax.ppermute(total, both, pairs))]
  transfers between devices with their start and end apart: 8 -> 11, of which waited for: 3 -> 6; matrix products, arithmetic and copies ran while one was open for 3% -> 2% of each run, Pallas kernels for 41% -> 10%
where the time goes in v2:
time: 33.8 us; the launch traced here: 33.4 us
  Pallas kernels  16.2 us (48%)
  starting transfers between devices  10.2 us (30%)
  waiting for transfers between devices  4.51 us (13%)
  local copies, waits for them, and re-layouts  1.16 us (3%)
  other arithmetic  0.67 us (2%)
  between operations  0.66 us (2%)
    ppermute x6, starting transfers between devices, all_tallies(): received.append(lax.ppermute(total, both, pairs))  8.73 us
    pallas_call x1, Pallas kernels, place(): pl.pallas_call(place_body, in_specs=[pl.BlockSpec(memory_space=pltpu.SMEM...  7 us
    pallas_call x1, Pallas kernels, on_device(): pl.pallas_call(lambda *refs: second_body(spans, pillars, sub_of, *refs),...  4.49 us
    pallas_call x1, Pallas kernels, on_device(): pl.pallas_call(lambda *refs: first_body(own_span, pillars, *refs), in_spe...  3.29 us
    ppermute x6, waiting for transfers between devices, all_tallies(): received.append(lax.ppermute(total, both, pairs))  3.03 us
    pallas_call x1, Pallas kernels, on_device(): pl.pallas_call(lambda *refs: tally_body(lambda c, t: live_points(own_span...  1.38 us
    ppermute x4, starting transfers between devices, on_device(): others.extend((lax.ppermute(x, 'bev', pairs) for x in own))  1.01 us
    ppermute x1, waiting for transfers between devices, all_tallies(): total = total + lax.ppermute(tally, 'bev', pairs)  0.95 us
  transfers between devices with their start and end apart: 11, of which 6 were waited for; matrix products, arithmetic and copies ran while one was open for 2% of the time, Pallas kernels for 10%

profile of v2, /device:TPU:0, one launch (start us, length us, event | category | flops | bytes accessed | tf_op | source)
XLA Modules:
  0.0 33.4 jit_solution(11088546834921554084)
XLA Ops:
  0.6 1.4 %tally.1 = f32[1,128]{1,0:T(1,128)} custom-call(s32[16]{0:T(128)} %refs_0_.5, s32[1,4096]{1,0:T(1,128)} %bitcast.12), custom_call_target="tpu_custom_call" | custom-call | tf_op jit(solution)/shard_map/tally/pallas_call | solution.py:378
  2.0 0.5 %collective-permute-start.4 = (f32[1,128]{1,0:T(1,128)}, f32[1,128]{1,0:T(1,128)S(1)}, u32[]{:S(2)}, u32[]{:S(2)}) collective-permute-start(f32[1,128]{1,0:T(1,128)} %tally.1), channel_id=1, source_target_pairs={{1,0},{0,1},{3,2},{2,3},{5,4},{4,5},{7,6},{6,7},{9,8},{8,9},{11,10... | collective-permute-start | bytes 1544 | tf_op jit(solution)/shard_map/ppermute | solution.py:312
  2.5 1.0 %collective-permute-done.4 = f32[1,128]{1,0:T(1,128)S(1)} collective-permute-done((f32[1,128]{1,0:T(1,128)}, f32[1,128]{1,0:T(1,128)S(1)}, u32[]{:S(2)}, u32[]{:S(2)}) %collective-permute-start.4) | collective-permute-done | bytes 544 | tf_op jit(solution)/shard_map/ppermute | solution.py:312
  3.5 0.7 %add.21 = f32[1,128]{1,0:T(1,128)S(1)} add(f32[1,128]{1,0:T(1,128)} %tally.1, f32[1,128]{1,0:T(1,128)S(1)} %collective-permute-done.4) | non-fusion elementwise | flops 128 | bytes 1536 | tf_op jit(solution)/shard_map/add | solution.py:312
  4.1 3.8 %collective-permute-start.7 = (f32[1,128]{1,0:T(1,128)S(1)}, f32[1,128]{1,0:T(1,128)S(1)}, u32[]{:S(2)}, u32[]{:S(2)}) collective-permute-start(f32[1,128]{1,0:T(1,128)S(1)} %add.21), channel_id=1, source_target_pairs={{0,6},{1,7},{2,4},{3,5},{4,2},{5,3},{6,0},{7,1},{8,14},{9,15},{10,... | collective-permute-start | bytes 1544 | tf_op jit(solution)/shard_map/ppermute | solution.py:325
  7.9 0.5 %collective-permute-start.5 = (f32[1,128]{1,0:T(1,128)S(1)}, f32[1,128]{1,0:T(1,128)S(1)}, u32[]{:S(2)}, u32[]{:S(2)}) collective-permute-start(f32[1,128]{1,0:T(1,128)S(1)} %add.21), channel_id=1, source_target_pairs={{0,2},{1,3},{2,0},{3,1},{4,6},{5,7},{6,4},{7,5},{8,10},{9,11},{10,... | collective-permute-start | bytes 1544 | tf_op jit(solution)/shard_map/ppermute | solution.py:325
  8.4 0.0 collective-permute-start.6
  8.5 0.0 collective-permute-start.1
  8.5 0.5 %collective-permute-start = (f32[4,4096]{1,0:T(4,128)}, f32[4,4096]{1,0:T(4,128)S(1)}, u32[]{:S(2)}, u32[]{:S(2)}) collective-permute-start(f32[4,4096]{1,0:T(4,128)} %refs_4_.1), channel_id=1, source_target_pairs={{1,0},{0,1},{3,2},{2,3},{5,4},{4,5},{7,6},{6,7},{9,8},{8,9},{11,10... | collective-permute-start | bytes 196616 | tf_op jit(solution)/shard_map/ppermute | solution.py:364
  9.0 0.5 %collective-permute-done.7 = f32[1,128]{1,0:T(1,128)S(1)} collective-permute-done((f32[1,128]{1,0:T(1,128)S(1)}, f32[1,128]{1,0:T(1,128)S(1)}, u32[]{:S(2)}, u32[]{:S(2)}) %collective-permute-start.7) | collective-permute-done | bytes 544 | tf_op jit(solution)/shard_map/ppermute | solution.py:325
  9.4 2.0 %collective-permute-done.5 = f32[1,128]{1,0:T(1,128)S(1)} collective-permute-done((f32[1,128]{1,0:T(1,128)S(1)}, f32[1,128]{1,0:T(1,128)S(1)}, u32[]{:S(2)}, u32[]{:S(2)}) %collective-permute-start.5) | collective-permute-done | bytes 544 | tf_op jit(solution)/shard_map/ppermute | solution.py:325
  11.5 0.5 %collective-permute-done.6 = f32[1,128]{1,0:T(1,128)S(1)} collective-permute-done((f32[1,128]{1,0:T(1,128)S(1)}, f32[1,128]{1,0:T(1,128)S(1)}, u32[]{:S(2)}, u32[]{:S(2)}) %collective-permute-start.6) | collective-permute-done | bytes 544 | tf_op jit(solution)/shard_map/ppermute | solution.py:325
  12.0 3.6 %collective-permute-start.10 = (f32[1,128]{1,0:T(1,128)S(1)}, f32[1,128]{1,0:T(1,128)S(1)}, u32[]{:S(2)}, u32[]{:S(2)}) collective-permute-start(f32[1,128]{1,0:T(1,128)S(1)} %add_add_fusion), channel_id=1, source_target_pairs={{0,24},{1,25},{2,26},{3,27},{4,28},{5,29},{6,30},{7,31},{8,16},{9,... | collective-permute-start | bytes 1544 | tf_op jit(solution)/shard_map/ppermute | solution.py:325
  15.6 0.0 collective-permute-start.8
  15.6 0.8 %collective-permute-start.9 = (f32[1,128]{1,0:T(1,128)S(1)}, f32[1,128]{1,0:T(1,128)S(1)}, u32[]{:S(2)}, u32[]{:S(2)}) collective-permute-start(f32[1,128]{1,0:T(1,128)S(1)} %add_add_fusion), channel_id=1, source_target_pairs={{0,16},{1,17},{2,18},{3,19},{4,20},{5,21},{6,22},{7,23},{8,24},{9,... | collective-permute-start | bytes 1544 | tf_op jit(solution)/shard_map/ppermute | solution.py:325
  16.4 3.3 %pool_own.1 = (f32[400,256]{1,0:T(8,128)}, bf16[64,80]{1,0:T(8,128)(2,1)}) custom-call(s32[16]{0:T(128)} %refs_0_.5, f32[11,11]{1,0:T(8,128)} %refs_1_.1, f32[15,64]{1,0:T(8,128)} %bitcast.19, f32[1,64]{1,0:T(1,128)} %bitcast.21, f32[4,4096]{1,0:T(4,128)} %refs_4_.1, s32[1,4096]{1,0:T(1,128)} %bitcast.14, s32[1,4096]{1,0:T(1,128)} %bitcast.15, ...), custom_call_target="tpu_custom_call" | custom-call | flops 1000000000 | bytes 1000000 | tf_op jit(solution)/shard_map/pool_own/pallas_call | solution.py:387
  19.7 0.0 collective-permute-done.10
  19.7 0.0 collective-permute-start.2
  19.7 0.0 collective-permute-done.8
  19.7 0.5 %collective-permute-start.3 = (s32[1,4096]{1,0:T(1,128)}, s32[1,4096]{1,0:T(1,128)S(1)}, u32[]{:S(2)}, u32[]{:S(2)}) collective-permute-start(s32[1,4096]{1,0:T(1,128)} %bitcast.18), channel_id=1, source_target_pairs={{1,0},{0,1},{3,2},{2,3},{5,4},{4,5},{7,6},{6,7},{9,8},{8,9},{11,10... | collective-permute-start | bytes 49160 | tf_op jit(solution)/shard_map/ppermute | solution.py:364
  20.2 0.0 collective-permute-done.9
  20.2 0.5 %slice_bitcast_fusion = f32[11]{0:T(128)} fusion(f32[1,128]{1,0:T(1,128)S(1)} %add_multiply_fusion), kind=kLoop, calls=%fused_computation | loop fusion | bytes 88 | tf_op jit(solution)/shard_map/squeeze | solution.py:385
  20.7 0.0 collective-permute-done.1.refs_5_
  20.7 0.0 copy-start.1
  20.7 0.3 %collective-permute-done.2.refs_6_ = s32[1,4096]{1,0:T(1,128)S(1)} collective-permute-done((s32[1,4096]{1,0:T(1,128)}, s32[1,4096]{1,0:T(1,128)S(1)}, u32[]{:S(2)}, u32[]{:S(2)}) %collective-permute-start.2) | collective-permute-done | bytes 16416 | tf_op jit(solution)/shard_map/ppermute | solution.py:364
  21.1 0.0 copy-start.2
  21.1 0.2 collective-permute-done.3.refs_7_
  21.2 0.0 copy-start.3
  21.2 0.0 collective-permute-done.refs_4_
  21.2 0.0 copy-start
  21.2 0.1 copy-done.1
  21.3 0.4 %copy-done.2 = s32[1,4096]{1,0:T(1,128)} copy-done((s32[1,4096]{1,0:T(1,128)}, s32[1,4096]{1,0:T(1,128)S(1)}, u32[]{:S(2)}) %copy-start.2) | copy-done | bytes 16408
  21.7 0.2 copy-done.3
  21.8 0.1 copy-done
  21.9 4.5 %pool_rest.1 = (f32[14,72,128]{2,1,0:T(8,128)}, s32[1,128]{1,0:T(1,128)}) custom-call(s32[16]{0:T(128)} %refs_0_.5, bf16[64,80]{1,0:T(8,128)(2,1)} %get-tuple-element.6.refs_1_, f32[400,256]{1,0:T(8,128)} %get-tuple-element.7.refs_2_, s32[1,1500]{1,0:T(1,128)} %bitcast.20, f32[4,4096]{1,0:T(4,128)} %copy-done, s32[1,4096]{1,0:T(1,128)} %copy-done.1, ...), custom_call_target="tpu_custom_call" | custom-call | flops 1000000000 | bytes 1000000 | tf_op jit(solution)/shard_map/pool_rest/pallas_call | solution.py:404
  26.4 7.0 %place.1 = bf16[64,432,248]{2,1,0:T(8,128)(2,1)} custom-call(s32[1,128]{1,0:T(1,128)} %get-tuple-element.8.starts_ref, f32[14,72,128]{2,1,0:T(8,128)} %get-tuple-element.9.sorted_ref), custom_call_target="tpu_custom_call" | custom-call | flops 1000000000 | bytes 10000000 | tf_op jit(solution)/shard_map/place/pallas_call | solution.py:287
  (2 shorter events, 0.0 us)
Async XLA Ops:
  2.0 1.4 %collective-permute-start.4 = (f32[1,128]{1,0:T(1,128)}, f32[1,128]{1,0:T(1,128)S(1)}, u32[]{:S(2)}, u32[]{:S(2)}) collective-permute-start(f32[1,128]{1,0:T(1,128)} %tally.1), channel_id=1, source_target_pairs={{1,0},{0,1},{3,2},{2,3},{5,4},{4,5},{7,6},{6,7},{9,8},{8,9},{11,10... | collective-permute-start | bytes 1544 | tf_op jit(solution)/shard_map/ppermute | solution.py:312
  4.1 5.3 %collective-permute-start.7 = (f32[1,128]{1,0:T(1,128)S(1)}, f32[1,128]{1,0:T(1,128)S(1)}, u32[]{:S(2)}, u32[]{:S(2)}) collective-permute-start(f32[1,128]{1,0:T(1,128)S(1)} %add.21), channel_id=1, source_target_pairs={{0,6},{1,7},{2,4},{3,5},{4,2},{5,3},{6,0},{7,1},{8,14},{9,15},{10,... | collective-permute-start | bytes 1544 | tf_op jit(solution)/shard_map/ppermute | solution.py:325
  7.9 3.6 %collective-permute-start.5 = (f32[1,128]{1,0:T(1,128)S(1)}, f32[1,128]{1,0:T(1,128)S(1)}, u32[]{:S(2)}, u32[]{:S(2)}) collective-permute-start(f32[1,128]{1,0:T(1,128)S(1)} %add.21), channel_id=1, source_target_pairs={{0,2},{1,3},{2,0},{3,1},{4,6},{5,7},{6,4},{7,5},{8,10},{9,11},{10,... | collective-permute-start | bytes 1544 | tf_op jit(solution)/shard_map/ppermute | solution.py:325
  8.4 3.6 %collective-permute-start.6 = (f32[1,128]{1,0:T(1,128)S(1)}, f32[1,128]{1,0:T(1,128)S(1)}, u32[]{:S(2)}, u32[]{:S(2)}) collective-permute-start(f32[1,128]{1,0:T(1,128)S(1)} %add.21), channel_id=1, source_target_pairs={{0,4},{1,5},{2,6},{3,7},{4,0},{5,1},{6,2},{7,3},{8,12},{9,13},{10,... | collective-permute-start | bytes 1544 | tf_op jit(solution)/shard_map/ppermute | solution.py:325
  8.5 12.3 %collective-permute-start.1 = (s32[1,4096]{1,0:T(1,128)}, s32[1,4096]{1,0:T(1,128)S(1)}, u32[]{:S(2)}, u32[]{:S(2)}) collective-permute-start(s32[1,4096]{1,0:T(1,128)} %bitcast.13), channel_id=1, source_target_pairs={{1,0},{0,1},{3,2},{2,3},{5,4},{4,5},{7,6},{6,7},{9,8},{8,9},{11,10... | collective-permute-start | bytes 49160 | tf_op jit(solution)/shard_map/ppermute | solution.py:364
  8.5 12.8 %collective-permute-start = (f32[4,4096]{1,0:T(4,128)}, f32[4,4096]{1,0:T(4,128)S(1)}, u32[]{:S(2)}, u32[]{:S(2)}) collective-permute-start(f32[4,4096]{1,0:T(4,128)} %refs_4_.1), channel_id=1, source_target_pairs={{1,0},{0,1},{3,2},{2,3},{5,4},{4,5},{7,6},{6,7},{9,8},{8,9},{11,10... | collective-permute-start | bytes 196616 | tf_op jit(solution)/shard_map/ppermute | solution.py:364
  12.0 7.7 %collective-permute-start.10 = (f32[1,128]{1,0:T(1,128)S(1)}, f32[1,128]{1,0:T(1,128)S(1)}, u32[]{:S(2)}, u32[]{:S(2)}) collective-permute-start(f32[1,128]{1,0:T(1,128)S(1)} %add_add_fusion), channel_id=1, source_target_pairs={{0,24},{1,25},{2,26},{3,27},{4,28},{5,29},{6,30},{7,31},{8,16},{9,... | collective-permute-start | bytes 1544 | tf_op jit(solution)/shard_map/ppermute | solution.py:325
  15.6 4.1 %collective-permute-start.8 = (f32[1,128]{1,0:T(1,128)S(1)}, f32[1,128]{1,0:T(1,128)S(1)}, u32[]{:S(2)}, u32[]{:S(2)}) collective-permute-start(f32[1,128]{1,0:T(1,128)S(1)} %add_add_fusion), channel_id=1, source_target_pairs={{0,8},{1,9},{2,10},{3,11},{4,12},{5,13},{6,14},{7,15},{8,0},{9,1},... | collective-permute-start | bytes 1544 | tf_op jit(solution)/shard_map/ppermute | solution.py:325
  15.6 4.6 %collective-permute-start.9 = (f32[1,128]{1,0:T(1,128)S(1)}, f32[1,128]{1,0:T(1,128)S(1)}, u32[]{:S(2)}, u32[]{:S(2)}) collective-permute-start(f32[1,128]{1,0:T(1,128)S(1)} %add_add_fusion), channel_id=1, source_target_pairs={{0,16},{1,17},{2,18},{3,19},{4,20},{5,21},{6,22},{7,23},{8,24},{9,... | collective-permute-start | bytes 1544 | tf_op jit(solution)/shard_map/ppermute | solution.py:325
  19.7 1.4 %collective-permute-start.2 = (s32[1,4096]{1,0:T(1,128)}, s32[1,4096]{1,0:T(1,128)S(1)}, u32[]{:S(2)}, u32[]{:S(2)}) collective-permute-start(s32[1,4096]{1,0:T(1,128)} %bitcast.16), channel_id=1, source_target_pairs={{1,0},{0,1},{3,2},{2,3},{5,4},{4,5},{7,6},{6,7},{9,8},{8,9},{11,10... | collective-permute-start | bytes 49160 | tf_op jit(solution)/shard_map/ppermute | solution.py:364
  19.7 1.5 %collective-permute-start.3 = (s32[1,4096]{1,0:T(1,128)}, s32[1,4096]{1,0:T(1,128)S(1)}, u32[]{:S(2)}, u32[]{:S(2)}) collective-permute-start(s32[1,4096]{1,0:T(1,128)} %bitcast.18), channel_id=1, source_target_pairs={{1,0},{0,1},{3,2},{2,3},{5,4},{4,5},{7,6},{6,7},{9,8},{8,9},{11,10... | collective-permute-start | bytes 49160 | tf_op jit(solution)/shard_map/ppermute | solution.py:364
  20.7 0.6 %copy-start.1 = (s32[1,4096]{1,0:T(1,128)}, s32[1,4096]{1,0:T(1,128)S(1)}, u32[]{:S(2)}) copy-start(s32[1,4096]{1,0:T(1,128)S(1)} %collective-permute-done.1.refs_5_) | copy-start | bytes 49156
  21.1 0.6 %copy-start.2 = (s32[1,4096]{1,0:T(1,128)}, s32[1,4096]{1,0:T(1,128)S(1)}, u32[]{:S(2)}) copy-start(s32[1,4096]{1,0:T(1,128)S(1)} %collective-permute-done.2.refs_6_) | copy-start | bytes 49156
  21.2 0.6 %copy-start.3 = (s32[1,4096]{1,0:T(1,128)}, s32[1,4096]{1,0:T(1,128)S(1)}, u32[]{:S(2)}) copy-start(s32[1,4096]{1,0:T(1,128)S(1)} %collective-permute-done.3.refs_7_) | copy-start | bytes 49156
  21.2 0.6 %copy-start = (f32[4,4096]{1,0:T(4,128)}, f32[4,4096]{1,0:T(4,128)S(1)}, u32[]{:S(2)}) copy-start(f32[4,4096]{1,0:T(4,128)S(1)} %collective-permute-done.refs_4_) | copy-start | bytes 196612

commit v3 on v2

--- a/solution.py
+++ b/solution.py
@@ -13,7 +13,6 @@
 STEP = 16
 BUCKETS = 32
 GROUP = 3
-LEADER_ONLY = False
 HIGHEST = lax.Precision.HIGHEST
 NT = (((1,), (1,)), ((), ()))
 
@@ -75,14 +74,18 @@
     return tall, one_hot
 
 
-def tally_body(live_of, counts_ref, class_ref, tally_ref):
-    classes = class_ref[...]
-    live = live_of(counts_ref, classes.shape[1])
-    total = classes.shape[1]
-    one_hot = to_f32((iota((16, total), 0) == classes) & live)
-    tally = jnp.sum(one_hot, axis=1, keepdims=True)
+def class_tally(spans, counts_ref, class_refs):
+    tally = jnp.zeros((16, 128), jnp.float32)
+    for span, class_ref in zip(spans, class_refs):
+        classes = class_ref[...]
+        total = classes.shape[1]
+        live = live_points(span, counts_ref, total)
+        one_hot = to_f32((iota((16, total), 0) == classes) & live)
+        for begin in range(0, total, 128):
+            tally = tally + one_hot[:, begin : begin + 128]
+    tally = jnp.sum(tally, axis=1, keepdims=True)
     diagonal = iota((16, 128), 0) == iota((16, 128), 1)
-    tally_ref[...] = jnp.sum(jnp.where(diagonal, tally, 0.0), axis=0, keepdims=True)
+    return jnp.sum(jnp.where(diagonal, tally, 0.0), axis=0, keepdims=True)
 
 
 def live_points(span, counts_ref, total):
@@ -115,12 +118,14 @@
     )
 
 
-def first_body(span, pillars, counts_ref, scores_ref, weight_ref, bias_ref, *refs):
+def first_body(span, spans, pillars, counts_ref, scores_ref, weight_ref, bias_ref, *refs):
     hi_count = round_up(pillars, LO) // LO
-    sums_ref, matrix_ref = refs[4:]
+    own, other_classes = refs[:4], refs[4 : 4 + len(spans)]
+    sums_ref, matrix_ref, tally_ref = refs[4 + len(spans) :]
+    tally_ref[...] = class_tally([span, *spans], counts_ref, [own[1], *other_classes])
     matrix = encoder_matrix(weight_ref[...], scores_ref[...], bias_ref[...])
     matrix_ref[...] = matrix
-    sums_ref[...] = pool_part(span, hi_count, matrix, counts_ref, *refs[:4])
+    sums_ref[...] = pool_part(span, hi_count, matrix, counts_ref, *own)
 
 
 def second_body(spans, pillars, sub_of, counts_ref, matrix_ref, sums_in_ref, cell_ref, *refs):
@@ -203,18 +208,22 @@
         sorted_ref[chunk, channels:, :] = jnp.full((8, 128), -1.0, jnp.float32)
 
 
-def place_body(starts_ref, sorted_ref, out_ref, image, lane_hot, acc_ref, sems):
+def place_body(starts_vmem, sorted_ref, out_ref, starts_ref, image, lane_hot, acc_ref, sem, sems):
+    fetch = pltpu.make_async_copy(starts_vmem, starts_ref, sem)
+    fetch.start()
+    fetch.wait()
     channels, _, lanes = out_ref.shape
     chunks, wide, _ = lane_hot.shape
     blocks = image.shape[1] // STEP
-    for chunk in range(chunks):
+
+    def hot_of(chunk):
         lane = sorted_ref[chunk, channels + 1 : channels + 2, :].astype(jnp.int32)
-        lane_hot[chunk] = to_f32(iota((wide, 128), 0) == lane).astype(jnp.bfloat16)
+        return to_f32(iota((wide, 128), 0) == lane).astype(jnp.bfloat16)
 
     def base_of(block):
         return starts_ref[0, block] >> 7
 
-    def partial(block, turn):
+    def partial(block, turn, ready=True):
         talls = []
         hots = []
         for half in range(2):
@@ -229,7 +238,7 @@
                     jnp.concatenate([row * mask_a, row * mask_b], axis=0).astype(jnp.bfloat16)
                 )
             talls.append(jnp.concatenate(tall, axis=0))
-            hots.append(lane_hot[chunk])
+            hots.append(lane_hot[chunk] if ready else hot_of(chunk))
         return lax.dot_general(
             jnp.concatenate(talls, axis=1),
             jnp.concatenate(hots, axis=1),
@@ -243,8 +252,11 @@
         image[:, rows, :] = tile[:, :, :lanes]
 
     spans = []
-    for begin in range(0, blocks, GROUP):
-        spans.append((begin, min(begin + GROUP, blocks)))
+    begin = 0
+    while begin < blocks:
+        end = min(begin + min(len(spans) + 1, GROUP), blocks)
+        spans.append((begin, end))
+        begin = end
     copies = []
     for index, (begin, end) in enumerate(spans):
         rows = pl.ds(begin * STEP, (end - begin) * STEP)
@@ -255,7 +267,11 @@
 
     @pl.when(spread == 0)
     def _():
-        for (begin, end), copy in zip(spans, copies):
+        put(0, partial(0, 0, ready=False))
+        copies[0].start()
+        for chunk in range(chunks):
+            lane_hot[chunk] = hot_of(chunk)
+        for (begin, end), copy in zip(spans[1:], copies[1:]):
             for block in range(begin, end):
                 put(block, partial(block, 0))
             copy.start()
@@ -265,11 +281,11 @@
         @pl.loop(0, blocks)
         def _(block):
             turns = (starts_ref[0, block + 1] - base_of(block) * 128 + LO - 1) // LO
-            acc_ref[...] = partial(block, 0)
+            acc_ref[...] = partial(block, 0, ready=False)
 
             @pl.loop(1, turns)
             def _(turn):
-                acc_ref[...] += partial(block, turn)
+                acc_ref[...] += partial(block, turn, ready=False)
 
             put(pl.multiple_of(block, 1), acc_ref[...])
 
@@ -283,55 +299,41 @@
 def place(sorted_values, starts, channels, subs, lanes):
     wide = round_up(lanes, 128)
     blocks = pl.cdiv(subs, STEP)
-    groups = pl.cdiv(blocks, GROUP)
     return pl.pallas_call(
         place_body,
         in_specs=[
-            pl.BlockSpec(memory_space=pltpu.SMEM),
+            pl.BlockSpec(memory_space=pltpu.VMEM),
             pl.BlockSpec(memory_space=pltpu.VMEM),
         ],
         out_specs=pl.BlockSpec(memory_space=pl.ANY),
         scratch_shapes=[
+            pltpu.SMEM((1, 128), jnp.int32),
             pltpu.VMEM((channels, blocks * STEP, lanes), jnp.bfloat16),
             pltpu.VMEM((sorted_values.shape[0], wide, 128), jnp.bfloat16),
             pltpu.VMEM((channels * STEP, wide), jnp.float32),
-            pltpu.SemaphoreType.DMA((groups,)),
+            pltpu.SemaphoreType.DMA,
+            pltpu.SemaphoreType.DMA((blocks,)),
         ],
         out_shape=jax.ShapeDtypeStruct((channels, blocks * STEP, lanes), jnp.bfloat16),
         cost_estimate=pl.CostEstimate(flops=10**9, transcendentals=0, bytes_accessed=10**7),
         name="place",
-    )(starts, sorted_values)[:, :subs]
-
-
-def all_tallies(tally, frames, band_count):
-    both = ("pts", "bev")
-    leader = band_count - 1
-    total = tally
-    for shift in range(1, band_count):
-        pairs = [((i + shift) % band_count, i) for i in range(band_count)]
-        total = total + lax.ppermute(tally, "bev", pairs)
+    )(in_vmem(starts), in_vmem(sorted_values))[:, :subs]
+
+
+def in_vmem(value):
+    return pltpu.with_memory_space_constraint(value, pltpu.VMEM)
+
+
+def all_tallies(total, frames):
     stride = 1
     while stride < frames:
         radix = 4 if frames % (stride * 4) == 0 else 2
         received = []
         for hop in range(1, radix):
-            pairs = []
-            for i in range(frames):
-                j = i ^ (hop * stride)
-                if LEADER_ONLY:
-                    pairs.append((i * band_count + leader, j * band_count + leader))
-                else:
-                    pairs.extend((i * band_count + k, j * band_count + k) for k in range(band_count))
-            received.append(lax.ppermute(total, both, pairs))
+            pairs = [(i, i ^ (hop * stride)) for i in range(frames)]
+            received.append(lax.ppermute(total, "pts", pairs))
         total = total + sum(received)
         stride *= radix
-    if LEADER_ONLY:
-        given = [
-            lax.ppermute(total, "bev", [(leader, k)])
-            for k in range(band_count)
-            if k != leader
-        ]
-        total = jnp.where(lax.axis_index("bev") == leader, total, sum(given))
     return total
 
 
@@ -358,10 +360,17 @@
         point_band.reshape(1, -1),
         point_pillar.reshape(1, -1),
     )
+    shifts = [
+        [((i + shift) % band_count, i) for i in range(band_count)]
+        for shift in range(1, band_count)
+    ]
+    other_classes = [in_vmem(lax.ppermute(own[1], "bev", pairs)) for pairs in shifts]
     others = []
-    for shift in range(1, band_count):
-        pairs = [((i + shift) % band_count, i) for i in range(band_count)]
-        others.extend(lax.ppermute(x, "bev", pairs) for x in own)
+    for pairs, classes in zip(shifts, other_classes):
+        band, pillar, feats = [
+            in_vmem(lax.ppermute(own[index], "bev", pairs)) for index in (2, 3, 0)
+        ]
+        others.extend((feats, classes, band, pillar))
     spans = [lambda band, k=k: (band + k) % band_count for k in range(1, band_count)]
 
     def own_span(band):
@@ -375,22 +384,15 @@
     width = round_up(pillars, LO)
     vmem = pl.BlockSpec(memory_space=pltpu.VMEM)
     smem = pl.BlockSpec(memory_space=pltpu.SMEM)
-    tally = pl.pallas_call(
-        lambda *refs: tally_body(lambda c, t: live_points(own_span, c, t), *refs),
-        in_specs=[smem, vmem],
-        out_specs=vmem,
-        out_shape=jax.ShapeDtypeStruct((1, 128), jnp.float32),
-        name="tally",
-    )(point_counts, own[1])
-    class_counts = (all_tallies(tally, frames, band_count) / total)[0, :CLASSES]
     hi_count = width // LO
-    sums, matrix = pl.pallas_call(
-        lambda *refs: first_body(own_span, pillars, *refs),
-        in_specs=[smem] + [vmem] * 7,
-        out_specs=(vmem, vmem),
+    sums, matrix, tally = pl.pallas_call(
+        lambda *refs: first_body(own_span, spans, pillars, *refs),
+        in_specs=[smem] + [vmem] * (7 + len(other_classes)),
+        out_specs=(vmem, vmem, vmem),
         out_shape=(
-            jax.ShapeDtypeStruct((hi_count * channels + 16, LO), jnp.float32),
-            jax.ShapeDtypeStruct((channels, 80), jnp.bfloat16),
+            pltpu.VMEM((hi_count * channels + 16, LO), jnp.float32),
+            pltpu.VMEM((channels, 80), jnp.bfloat16),
+            pltpu.VMEM((1, 128), jnp.float32),
         ),
         cost_estimate=pl.CostEstimate(flops=10**9, transcendentals=0, bytes_accessed=10**6),
         name="pool_own",
@@ -400,19 +402,27 @@
         encoder_weight.T,
         encoder_bias.reshape(1, channels),
         *own,
-    )
+        *other_classes,
+    )
+    class_counts = (all_tallies(tally, frames) / total)[0, :CLASSES]
     sorted_values, starts = pl.pallas_call(
         lambda *refs: second_body(spans, pillars, sub_of, *refs),
         in_specs=[smem] + [vmem] * (3 + len(others)),
         out_specs=(vmem, vmem),
         out_shape=(
-            jax.ShapeDtypeStruct(((width + LO) // 128, channels + 8, 128), jnp.float32),
-            jax.ShapeDtypeStruct((1, 128), jnp.int32),
+            pltpu.VMEM(((width + LO) // 128, channels + 8, 128), jnp.float32),
+            pltpu.VMEM((1, 128), jnp.int32),
         ),
         scratch_shapes=[pltpu.VMEM((1, width), jnp.int32)],
         cost_estimate=pl.CostEstimate(flops=10**9, transcendentals=0, bytes_accessed=10**6),
         name="pool_rest",
-    )(point_counts, matrix, sums, pillar_cell.reshape(1, pillars), *others)
+    )(
+        point_counts,
+        in_vmem(matrix),
+        in_vmem(sums),
+        pillar_cell.reshape(1, pillars),
+        *others,
+    )
     planes = place(sorted_values, starts, channels, subs, lanes)
     bev_image = planes.swapaxes(1, 2) if sub_of == "col" else planes
     return (bev_image[None], class_counts)

time: 33.8 us -> 31.7 us (0.938)
  Pallas kernels: 16.2 us -> 12.7 us
  waiting for transfers between devices: 4.51 us -> 7.66 us
  other arithmetic: 0.67 us -> 0.01 us
  local copies, waits for them, and re-layouts: 1.16 us -> 0.51 us
    ppermute x11 -> x10, waiting for transfers between devices: 4.51 us -> 7.66 us  [the longest x6 6.6 us: all_tallies(): received.append(lax.ppermute(total, 'pts', pairs))]
    pallas_call x3 -> x2, Pallas kernels: 11.7 us -> 9.33 us  [the longest x1 6.76 us: place(): pl.pallas_call(place_body, in_specs=[pl.BlockSpec(memory_space=pltpu.VMEM...]
    pallas_call x1, Pallas kernels: 4.49 us -> 3.39 us  [on_device(): pl.pallas_call(lambda *refs: second_body(spans, pillars, sub_of, *refs),...]
    add x1 -> x0, other arithmetic: 0.66 us -> none  [all_tallies(): total = total + lax.ppermute(tally, 'bev', pairs)]
    unnamed x8 -> x0, local copies, waits for them, and re-layouts: 0.65 us -> none
    ppermute x11 -> x10, starting transfers between devices: 10.2 us -> 9.94 us  [the longest x6 8.87 us: all_tallies(): received.append(lax.ppermute(total, 'pts', pairs))]
  transfers between devices with their start and end apart: 11 -> 10, of which waited for: 6 -> 6; matrix products, arithmetic and copies ran while one was open for 2% -> 2% of each run, Pallas kernels for 10% -> 0%
where the time goes in v3:
time: 31.7 us; the launch traced here: 31.5 us
  Pallas kernels  12.7 us (40%)
  starting transfers between devices  9.94 us (31%)
  waiting for transfers between devices  7.66 us (24%)
  between operations  0.66 us (2%)
  local copies, waits for them, and re-layouts  0.51 us (2%)
    ppermute x6, starting transfers between devices, all_tallies(): received.append(lax.ppermute(total, 'pts', pairs))  8.87 us
    pallas_call x1, Pallas kernels, place(): pl.pallas_call(place_body, in_specs=[pl.BlockSpec(memory_space=pltpu.VMEM...  6.76 us
    ppermute x6, waiting for transfers between devices, all_tallies(): received.append(lax.ppermute(total, 'pts', pairs))  6.6 us
    pallas_call x1, Pallas kernels, on_device(): pl.pallas_call(lambda *refs: second_body(spans, pillars, sub_of, *refs),...  3.39 us
    pallas_call x1, Pallas kernels, on_device(): pl.pallas_call(lambda *refs: first_body(own_span, spans, pillars, *refs),...  2.57 us
    ppermute x1, waiting for transfers between devices, on_device(): lax.ppermute(own[1], 'bev', pairs)  1.05 us
  transfers between devices with their start and end apart: 10, of which 6 were waited for; matrix products, arithmetic and copies ran while one was open for 2% of the time, Pallas kernels for 0%

profile of v3, /device:TPU:0, one launch (start us, length us, event | category | flops | bytes accessed | tf_op | source)
XLA Modules:
  0.0 31.5 jit_solution(10141941992847783282)
XLA Ops:
  0.6 0.6 %collective-permute-start = (s32[1,4096]{1,0:T(1,128)}, s32[1,4096]{1,0:T(1,128)S(1)}, u32[]{:S(2)}, u32[]{:S(2)}) collective-permute-start(s32[1,4096]{1,0:T(1,128)} %bitcast.12), channel_id=1, source_target_pairs={{1,0},{0,1},{3,2},{2,3},{5,4},{4,5},{7,6},{6,7},{9,8},{8,9},{11,10... | collective-permute-start | bytes 49160 | tf_op jit(solution)/shard_map/ppermute | solution.py:367
  1.2 1.0 %collective-permute-done.refs_8_.refs_5_ = s32[1,4096]{1,0:T(1,128)S(1)} collective-permute-done((s32[1,4096]{1,0:T(1,128)}, s32[1,4096]{1,0:T(1,128)S(1)}, u32[]{:S(2)}, u32[]{:S(2)}) %collective-permute-start) | collective-permute-done | bytes 16416 | tf_op jit(solution)/shard_map/ppermute | solution.py:367
  2.2 2.6 %pool_own.1 = (f32[400,256]{1,0:T(8,128)S(1)}, bf16[64,80]{1,0:T(8,128)(2,1)S(1)}, f32[1,128]{1,0:T(1,128)S(1)}) custom-call(s32[16]{0:T(128)} %refs_0_.3, f32[11,11]{1,0:T(8,128)} %refs_1_.1, f32[15,64]{1,0:T(8,128)} %bitcast.18, f32[1,64]{1,0:T(1,128)} %bitcast.20, f32[4,4096]{1,0:T(4,128)} %refs_4_.1, s32[1,4096]{1,0:T(1,128)} %bitcast.13, ...), custom_call_target="tpu_custom_call" | custom-call | flops 1000000000 | bytes 1000000 | tf_op jit(solution)/shard_map/pool_own/pallas_call | solution.py:388
  4.8 3.8 %collective-permute-start.6 = (f32[1,128]{1,0:T(1,128)S(1)}, f32[1,128]{1,0:T(1,128)S(1)}, u32[]{:S(2)}, u32[]{:S(2)}) collective-permute-start(f32[1,128]{1,0:T(1,128)S(1)} %get-tuple-element.11), channel_id=1, source_target_pairs={{0,6},{2,4},{4,2},{6,0},{8,14},{10,12},{12,10},{14,8},{16,22},{18,... | collective-permute-start | bytes 1544 | tf_op jit(solution)/shard_map/ppermute | solution.py:334
  8.6 0.5 %collective-permute-start.5 = (f32[1,128]{1,0:T(1,128)S(1)}, f32[1,128]{1,0:T(1,128)S(1)}, u32[]{:S(2)}, u32[]{:S(2)}) collective-permute-start(f32[1,128]{1,0:T(1,128)S(1)} %get-tuple-element.11), channel_id=1, source_target_pairs={{0,4},{2,6},{4,0},{6,2},{8,12},{10,14},{12,8},{14,10},{16,20},{18,... | collective-permute-start | bytes 1544 | tf_op jit(solution)/shard_map/ppermute | solution.py:334
  9.2 0.1 collective-permute-start.4
  9.3 0.9 %collective-permute-done.6 = f32[1,128]{1,0:T(1,128)S(1)} collective-permute-done((f32[1,128]{1,0:T(1,128)S(1)}, f32[1,128]{1,0:T(1,128)S(1)}, u32[]{:S(2)}, u32[]{:S(2)}) %collective-permute-start.6) | collective-permute-done | bytes 544 | tf_op jit(solution)/shard_map/ppermute | solution.py:334
  10.2 2.0 %collective-permute-done.5 = f32[1,128]{1,0:T(1,128)S(1)} collective-permute-done((f32[1,128]{1,0:T(1,128)S(1)}, f32[1,128]{1,0:T(1,128)S(1)}, u32[]{:S(2)}, u32[]{:S(2)}) %collective-permute-start.5) | collective-permute-done | bytes 544 | tf_op jit(solution)/shard_map/ppermute | solution.py:334
  12.2 0.5 %collective-permute-done.4 = f32[1,128]{1,0:T(1,128)S(1)} collective-permute-done((f32[1,128]{1,0:T(1,128)S(1)}, f32[1,128]{1,0:T(1,128)S(1)}, u32[]{:S(2)}, u32[]{:S(2)}) %collective-permute-start.4) | collective-permute-done | bytes 544 | tf_op jit(solution)/shard_map/ppermute | solution.py:334
  12.7 3.6 %collective-permute-start.9 = (f32[1,128]{1,0:T(1,128)S(1)}, f32[1,128]{1,0:T(1,128)S(1)}, u32[]{:S(2)}, u32[]{:S(2)}) collective-permute-start(f32[1,128]{1,0:T(1,128)S(1)} %add_add_fusion), channel_id=1, source_target_pairs={{0,24},{2,26},{4,28},{6,30},{8,16},{10,18},{12,20},{14,22},{16,8},... | collective-permute-start | bytes 1544 | tf_op jit(solution)/shard_map/ppermute | solution.py:334
  16.3 0.0 collective-permute-start.8
  16.3 0.8 %collective-permute-start.7 = (f32[1,128]{1,0:T(1,128)S(1)}, f32[1,128]{1,0:T(1,128)S(1)}, u32[]{:S(2)}, u32[]{:S(2)}) collective-permute-start(f32[1,128]{1,0:T(1,128)S(1)} %add_add_fusion), channel_id=1, source_target_pairs={{0,8},{2,10},{4,12},{6,14},{8,0},{10,2},{12,4},{14,6},{16,24},{18,... | collective-permute-start | bytes 1544 | tf_op jit(solution)/shard_map/ppermute | solution.py:334
  17.1 0.0 collective-permute-start.2
  17.1 0.5 %collective-permute-start.3 = (s32[1,4096]{1,0:T(1,128)}, s32[1,4096]{1,0:T(1,128)S(1)}, u32[]{:S(2)}, u32[]{:S(2)}) collective-permute-start(s32[1,4096]{1,0:T(1,128)} %bitcast.17), channel_id=1, source_target_pairs={{1,0},{0,1},{3,2},{2,3},{5,4},{4,5},{7,6},{6,7},{9,8},{8,9},{11,10... | collective-permute-start | bytes 49160 | tf_op jit(solution)/shard_map/ppermute | solution.py:371
  17.6 0.5 %collective-permute-done.9 = f32[1,128]{1,0:T(1,128)S(1)} collective-permute-done((f32[1,128]{1,0:T(1,128)S(1)}, f32[1,128]{1,0:T(1,128)S(1)}, u32[]{:S(2)}, u32[]{:S(2)}) %collective-permute-start.9) | collective-permute-done | bytes 544 | tf_op jit(solution)/shard_map/ppermute | solution.py:334
  18.1 0.0 collective-permute-start.1
  18.1 2.7 %collective-permute-done.8 = f32[1,128]{1,0:T(1,128)S(1)} collective-permute-done((f32[1,128]{1,0:T(1,128)S(1)}, f32[1,128]{1,0:T(1,128)S(1)}, u32[]{:S(2)}, u32[]{:S(2)}) %collective-permute-start.8) | collective-permute-done | bytes 544 | tf_op jit(solution)/shard_map/ppermute | solution.py:334
  20.8 0.0 collective-permute-done.7
  20.8 0.5 %slice_bitcast_fusion = f32[11]{0:T(128)} fusion(f32[1,128]{1,0:T(1,128)S(1)} %add_multiply_fusion), kind=kLoop, calls=%fused_computation | loop fusion | bytes 88 | tf_op jit(solution)/shard_map/squeeze | solution.py:407
  21.3 0.0 collective-permute-done.2.refs_6_
  21.3 0.0 collective-permute-done.3.refs_7_
  21.3 0.0 collective-permute-done.1.refs_4_
  21.3 3.4 %pool_rest.1 = (f32[14,72,128]{2,1,0:T(8,128)S(1)}, s32[1,128]{1,0:T(1,128)S(1)}) custom-call(s32[16]{0:T(128)} %refs_0_.3, bf16[64,80]{1,0:T(8,128)(2,1)S(1)} %get-tuple-element.7.refs_1_, f32[400,256]{1,0:T(8,128)S(1)} %get-tuple-element.8.refs_2_, s32[1,1500]{1,0:T(1,128)} %bitcast.19, f32[4,4096]{1,0:T(4,128)S(1)} %collective-permute-done.1.refs_4_, ...), custom_call_target="tpu_custom_call" | custom-call | flops 1000000000 | bytes 1000000 | tf_op jit(solution)/shard_map/pool_rest/pallas_call | solution.py:408
  24.7 6.8 %place.1 = bf16[64,432,248]{2,1,0:T(8,128)(2,1)} custom-call(s32[1,128]{1,0:T(1,128)S(1)} %get-tuple-element.9.starts_vmem, f32[14,72,128]{2,1,0:T(8,128)S(1)} %get-tuple-element.10.sorted_ref), custom_call_target="tpu_custom_call" | custom-call | flops 1000000000 | bytes 10000000 | tf_op jit(solution)/shard_map/place/pallas_call | solution.py:302
  (2 shorter events, 0.0 us)
Async XLA Ops:
  0.6 1.6 %collective-permute-start = (s32[1,4096]{1,0:T(1,128)}, s32[1,4096]{1,0:T(1,128)S(1)}, u32[]{:S(2)}, u32[]{:S(2)}) collective-permute-start(s32[1,4096]{1,0:T(1,128)} %bitcast.12), channel_id=1, source_target_pairs={{1,0},{0,1},{3,2},{2,3},{5,4},{4,5},{7,6},{6,7},{9,8},{8,9},{11,10... | collective-permute-start | bytes 49160 | tf_op jit(solution)/shard_map/ppermute | solution.py:367
  4.8 5.4 %collective-permute-start.6 = (f32[1,128]{1,0:T(1,128)S(1)}, f32[1,128]{1,0:T(1,128)S(1)}, u32[]{:S(2)}, u32[]{:S(2)}) collective-permute-start(f32[1,128]{1,0:T(1,128)S(1)} %get-tuple-element.11), channel_id=1, source_target_pairs={{0,6},{2,4},{4,2},{6,0},{8,14},{10,12},{12,10},{14,8},{16,22},{18,... | collective-permute-start | bytes 1544 | tf_op jit(solution)/shard_map/ppermute | solution.py:334
  8.6 3.6 %collective-permute-start.5 = (f32[1,128]{1,0:T(1,128)S(1)}, f32[1,128]{1,0:T(1,128)S(1)}, u32[]{:S(2)}, u32[]{:S(2)}) collective-permute-start(f32[1,128]{1,0:T(1,128)S(1)} %get-tuple-element.11), channel_id=1, source_target_pairs={{0,4},{2,6},{4,0},{6,2},{8,12},{10,14},{12,8},{14,10},{16,20},{18,... | collective-permute-start | bytes 1544 | tf_op jit(solution)/shard_map/ppermute | solution.py:334
  9.2 3.6 %collective-permute-start.4 = (f32[1,128]{1,0:T(1,128)S(1)}, f32[1,128]{1,0:T(1,128)S(1)}, u32[]{:S(2)}, u32[]{:S(2)}) collective-permute-start(f32[1,128]{1,0:T(1,128)S(1)} %get-tuple-element.11), channel_id=1, source_target_pairs={{0,2},{2,0},{4,6},{6,4},{8,10},{10,8},{12,14},{14,12},{16,18},{18,... | collective-permute-start | bytes 1544 | tf_op jit(solution)/shard_map/ppermute | solution.py:334
  12.7 5.4 %collective-permute-start.9 = (f32[1,128]{1,0:T(1,128)S(1)}, f32[1,128]{1,0:T(1,128)S(1)}, u32[]{:S(2)}, u32[]{:S(2)}) collective-permute-start(f32[1,128]{1,0:T(1,128)S(1)} %add_add_fusion), channel_id=1, source_target_pairs={{0,24},{2,26},{4,28},{6,30},{8,16},{10,18},{12,20},{14,22},{16,8},... | collective-permute-start | bytes 1544 | tf_op jit(solution)/shard_map/ppermute | solution.py:334
  16.3 4.5 %collective-permute-start.8 = (f32[1,128]{1,0:T(1,128)S(1)}, f32[1,128]{1,0:T(1,128)S(1)}, u32[]{:S(2)}, u32[]{:S(2)}) collective-permute-start(f32[1,128]{1,0:T(1,128)S(1)} %add_add_fusion), channel_id=1, source_target_pairs={{0,16},{2,18},{4,20},{6,22},{8,24},{10,26},{12,28},{14,30},{16,0},... | collective-permute-start | bytes 1544 | tf_op jit(solution)/shard_map/ppermute | solution.py:334
  16.3 4.5 %collective-permute-start.7 = (f32[1,128]{1,0:T(1,128)S(1)}, f32[1,128]{1,0:T(1,128)S(1)}, u32[]{:S(2)}, u32[]{:S(2)}) collective-permute-start(f32[1,128]{1,0:T(1,128)S(1)} %add_add_fusion), channel_id=1, source_target_pairs={{0,8},{2,10},{4,12},{6,14},{8,0},{10,2},{12,4},{14,6},{16,24},{18,... | collective-permute-start | bytes 1544 | tf_op jit(solution)/shard_map/ppermute | solution.py:334
  17.1 4.2 %collective-permute-start.2 = (s32[1,4096]{1,0:T(1,128)}, s32[1,4096]{1,0:T(1,128)S(1)}, u32[]{:S(2)}, u32[]{:S(2)}) collective-permute-start(s32[1,4096]{1,0:T(1,128)} %bitcast.15), channel_id=1, source_target_pairs={{1,0},{0,1},{3,2},{2,3},{5,4},{4,5},{7,6},{6,7},{9,8},{8,9},{11,10... | collective-permute-start | bytes 49160 | tf_op jit(solution)/shard_map/ppermute | solution.py:371
  17.1 4.2 %collective-permute-start.3 = (s32[1,4096]{1,0:T(1,128)}, s32[1,4096]{1,0:T(1,128)S(1)}, u32[]{:S(2)}, u32[]{:S(2)}) collective-permute-start(s32[1,4096]{1,0:T(1,128)} %bitcast.17), channel_id=1, source_target_pairs={{1,0},{0,1},{3,2},{2,3},{5,4},{4,5},{7,6},{6,7},{9,8},{8,9},{11,10... | collective-permute-start | bytes 49160 | tf_op jit(solution)/shard_map/ppermute | solution.py:371
  18.1 3.2 %collective-permute-start.1 = (f32[4,4096]{1,0:T(4,128)}, f32[4,4096]{1,0:T(4,128)S(1)}, u32[]{:S(2)}, u32[]{:S(2)}) collective-permute-start(f32[4,4096]{1,0:T(4,128)} %refs_4_.1), channel_id=1, source_target_pairs={{1,0},{0,1},{3,2},{2,3},{5,4},{4,5},{7,6},{6,7},{9,8},{8,9},{11,10... | collective-permute-start | bytes 196616 | tf_op jit(solution)/shard_map/ppermute | solution.py:371

commit v4 on v3

--- a/solution.py
+++ b/solution.py
@@ -89,7 +89,9 @@
 
 
 def live_points(span, counts_ref, total):
-    live_total = counts_ref[lax.axis_index("pts")]
+    counts = counts_ref[...]
+    mine = iota(counts.shape, 1) == lax.axis_index("pts")
+    live_total = jnp.sum(jnp.where(mine, counts, 0), axis=1, keepdims=True)
     return span(lax.axis_index("bev")) * total + iota((1, total), 1) < live_total
 
 
@@ -118,28 +120,9 @@
     )
 
 
-def first_body(span, spans, pillars, counts_ref, scores_ref, weight_ref, bias_ref, *refs):
-    hi_count = round_up(pillars, LO) // LO
-    own, other_classes = refs[:4], refs[4 : 4 + len(spans)]
-    sums_ref, matrix_ref, tally_ref = refs[4 + len(spans) :]
-    tally_ref[...] = class_tally([span, *spans], counts_ref, [own[1], *other_classes])
-    matrix = encoder_matrix(weight_ref[...], scores_ref[...], bias_ref[...])
-    matrix_ref[...] = matrix
-    sums_ref[...] = pool_part(span, hi_count, matrix, counts_ref, *own)
-
-
-def second_body(spans, pillars, sub_of, counts_ref, matrix_ref, sums_in_ref, cell_ref, *refs):
-    parts = len(spans)
-    sorted_ref, starts_ref, cell_pad = refs[4 * parts :]
-    channels = matrix_ref.shape[0]
+def order_pillars(pillars, sub_of, cell_ref, cell_pad, rank_ref, where_ref, starts_ref):
     hi_count = round_up(pillars, LO) // LO
     width = hi_count * LO
-    sums = sums_in_ref[...]
-    for part in range(parts):
-        sums = sums + pool_part(
-            spans[part], hi_count, matrix_ref[...], counts_ref, *refs[4 * part : 4 * part + 4]
-        )
-
     cell_pad[...] = jnp.full(cell_pad.shape, -1, jnp.int32)
     cell_pad[:, :pillars] = cell_ref[...].reshape(1, pillars)
     cell = cell_pad[...]
@@ -169,16 +152,14 @@
     wide = jnp.max(jnp.where(real, reach, 0), axis=1, keepdims=True) > LO
     starts_ref[...] = jnp.where(iota((1, 128), 1) == 127, wide.astype(jnp.int32), starts_i)
     start = jnp.sum(jnp.where(square == across, starts_row, 0.0), axis=1, keepdims=True)
-    placed = jnp.zeros((hi_count * (channels + 16), LO), jnp.float32)
     extra = iota((16, LO), 0)
-    counts = sums[hi_count * channels :]
     for h in range(hi_count):
         at = slice(h * LO, (h + 1) * LO)
-        rank = jnp.sum(member[:, at] * (ranks[h] + start), axis=0, keepdims=True).astype(jnp.int32)
-        mean = sums[h * channels : (h + 1) * channels] / jnp.maximum(counts[h : h + 1], 1.0)
+        rank = jnp.sum(member[:, at] * (ranks[h] + start), axis=0, keepdims=True)
+        rank_ref[:, at] = rank.astype(jnp.int32)
         sub_h = sub[:, at]
         lane_h = lane[:, at]
-        where = jnp.where(
+        where_ref[:, at] = jnp.where(
             extra == 0,
             block[:, at],
             jnp.where(
@@ -187,7 +168,49 @@
                 jnp.where(extra == 2, lane_h >> 8, jnp.where(extra == 3, lane_h & 255, 0)),
             ),
         ).astype(jnp.float32)
-        values = jnp.concatenate([mean, where], axis=0).astype(jnp.bfloat16)
+
+
+def first_body(
+    span, spans, pillars, sub_of, counts_ref, scores_ref, weight_ref, bias_ref, cell_ref, *refs
+):
+    hi_count = round_up(pillars, LO) // LO
+    own, other_classes = refs[:4], refs[4 : 4 + len(spans)]
+    (
+        sums_ref,
+        matrix_ref,
+        tally_ref,
+        counts_out,
+        rank_ref,
+        where_ref,
+        starts_ref,
+        cell_pad,
+    ) = refs[4 + len(spans) :]
+    counts_out[...] = counts_ref[...]
+    tally_ref[...] = class_tally([span, *spans], counts_ref, [own[1], *other_classes])
+    matrix = encoder_matrix(weight_ref[...], scores_ref[...], bias_ref[...])
+    matrix_ref[...] = matrix
+    sums_ref[...] = pool_part(span, hi_count, matrix, counts_ref, *own)
+    order_pillars(pillars, sub_of, cell_ref, cell_pad, rank_ref, where_ref, starts_ref)
+
+
+def second_body(spans, pillars, counts_ref, matrix_ref, sums_in_ref, rank_ref, where_ref, *refs):
+    parts = len(spans)
+    (sorted_ref,) = refs[4 * parts :]
+    channels = matrix_ref.shape[0]
+    hi_count = round_up(pillars, LO) // LO
+    sums = sums_in_ref[...]
+    for part in range(parts):
+        sums = sums + pool_part(
+            spans[part], hi_count, matrix_ref[...], counts_ref, *refs[4 * part : 4 * part + 4]
+        )
+
+    placed = jnp.zeros((hi_count * (channels + 16), LO), jnp.float32)
+    counts = sums[hi_count * channels :]
+    for h in range(hi_count):
+        at = slice(h * LO, (h + 1) * LO)
+        rank = rank_ref[:, at]
+        mean = sums[h * channels : (h + 1) * channels] / jnp.maximum(counts[h : h + 1], 1.0)
+        values = jnp.concatenate([mean, where_ref[:, at]], axis=0).astype(jnp.bfloat16)
         tall, lo_hot = two_level(values, rank >> 8, rank & (LO - 1), hi_count)
         placed = placed + lax.dot_general(
             jnp.concatenate(tall, axis=0), lo_hot, NT, preferred_element_type=jnp.float32
@@ -324,14 +347,18 @@
     return pltpu.with_memory_space_constraint(value, pltpu.VMEM)
 
 
-def all_tallies(total, frames):
+def all_tallies(total, frames, bands):
     stride = 1
     while stride < frames:
         radix = 4 if frames % (stride * 4) == 0 else 2
         received = []
         for hop in range(1, radix):
-            pairs = [(i, i ^ (hop * stride)) for i in range(frames)]
-            received.append(lax.ppermute(total, "pts", pairs))
+            pairs = [
+                (i * bands + k, (i ^ (hop * stride)) * bands + bands - 1 - k)
+                for i in range(frames)
+                for k in range(bands)
+            ]
+            received.append(lax.ppermute(total, ("pts", "bev"), pairs))
         total = total + sum(received)
         stride *= radix
     return total
@@ -383,46 +410,41 @@
     subs, lanes = (COLS, band_rows) if sub_of == "col" else (band_rows, COLS)
     width = round_up(pillars, LO)
     vmem = pl.BlockSpec(memory_space=pltpu.VMEM)
-    smem = pl.BlockSpec(memory_space=pltpu.SMEM)
     hi_count = width // LO
-    sums, matrix, tally = pl.pallas_call(
-        lambda *refs: first_body(own_span, spans, pillars, *refs),
-        in_specs=[smem] + [vmem] * (7 + len(other_classes)),
-        out_specs=(vmem, vmem, vmem),
+    sums, matrix, tally, counts, rank, where, starts = pl.pallas_call(
+        lambda *refs: first_body(own_span, spans, pillars, sub_of, *refs),
+        in_specs=[vmem] * (9 + len(other_classes)),
+        out_specs=(vmem,) * 7,
         out_shape=(
             pltpu.VMEM((hi_count * channels + 16, LO), jnp.float32),
             pltpu.VMEM((channels, 80), jnp.bfloat16),
             pltpu.VMEM((1, 128), jnp.float32),
-        ),
-        cost_estimate=pl.CostEstimate(flops=10**9, transcendentals=0, bytes_accessed=10**6),
-        name="pool_own",
-    )(
-        point_counts,
-        class_scores,
-        encoder_weight.T,
-        encoder_bias.reshape(1, channels),
-        *own,
-        *other_classes,
-    )
-    class_counts = (all_tallies(tally, frames) / total)[0, :CLASSES]
-    sorted_values, starts = pl.pallas_call(
-        lambda *refs: second_body(spans, pillars, sub_of, *refs),
-        in_specs=[smem] + [vmem] * (3 + len(others)),
-        out_specs=(vmem, vmem),
-        out_shape=(
-            pltpu.VMEM(((width + LO) // 128, channels + 8, 128), jnp.float32),
+            pltpu.VMEM((1, frames), jnp.int32),
+            pltpu.VMEM((1, width), jnp.int32),
+            pltpu.VMEM((16, width), jnp.float32),
             pltpu.VMEM((1, 128), jnp.int32),
         ),
         scratch_shapes=[pltpu.VMEM((1, width), jnp.int32)],
         cost_estimate=pl.CostEstimate(flops=10**9, transcendentals=0, bytes_accessed=10**6),
+        name="pool_own",
+    )(
+        point_counts.reshape(1, frames),
+        class_scores,
+        encoder_weight.T,
+        encoder_bias.reshape(1, channels),
+        pillar_cell.reshape(1, pillars),
+        *own,
+        *other_classes,
+    )
+    class_counts = (all_tallies(tally, frames, band_count) / total)[0, :CLASSES]
+    sorted_values = pl.pallas_call(
+        lambda *refs: second_body(spans, pillars, *refs),
+        in_specs=[vmem] * (5 + len(others)),
+        out_specs=vmem,
+        out_shape=pltpu.VMEM(((width + LO) // 128, channels + 8, 128), jnp.float32),
+        cost_estimate=pl.CostEstimate(flops=10**9, transcendentals=0, bytes_accessed=10**6),
         name="pool_rest",
-    )(
-        point_counts,
-        in_vmem(matrix),
-        in_vmem(sums),
-        pillar_cell.reshape(1, pillars),
-        *others,
-    )
+    )(*[in_vmem(x) for x in (counts, matrix, sums, rank, where)], *others)
     planes = place(sorted_values, starts, channels, subs, lanes)
     bev_image = planes.swapaxes(1, 2) if sub_of == "col" else planes
     return (bev_image[None], class_counts)

time: 31.7 us -> 29.3 us (0.924)
  waiting for transfers between devices: 7.66 us -> 6.54 us
  Pallas kernels: 12.7 us -> 12 us
  starting transfers between devices: 9.94 us -> 9.39 us
    ppermute x6, waiting for transfers between devices: 6.6 us -> 5.49 us  [all_tallies(): received.append(lax.ppermute(total, ('pts', 'bev'), pairs))]
    ppermute x6, starting transfers between devices: 8.87 us -> 8.15 us  [all_tallies(): received.append(lax.ppermute(total, ('pts', 'bev'), pairs))]
    pallas_call x2, Pallas kernels: 5.96 us -> 5.27 us  [the longest x1 2.77 us: on_device(): pl.pallas_call(lambda *refs: first_body(own_span, spans, pillars, sub_of,...]
where the time goes in v4:
time: 29.3 us; the launch traced here: 29.1 us
  Pallas kernels  12 us (41%)
  starting transfers between devices  9.39 us (32%)
  waiting for transfers between devices  6.54 us (22%)
  between operations  0.66 us (2%)
  local copies, waits for them, and re-layouts  0.51 us (2%)
    ppermute x6, starting transfers between devices, all_tallies(): received.append(lax.ppermute(total, ('pts', 'bev'), pairs))  8.15 us
    pallas_call x1, Pallas kernels, place(): pl.pallas_call(place_body, in_specs=[pl.BlockSpec(memory_space=pltpu.VMEM...  6.76 us
    ppermute x6, waiting for transfers between devices, all_tallies(): received.append(lax.ppermute(total, ('pts', 'bev'), pairs))  5.49 us
    pallas_call x1, Pallas kernels, on_device(): pl.pallas_call(lambda *refs: first_body(own_span, spans, pillars, sub_of,...  2.77 us
    pallas_call x1, Pallas kernels, on_device(): pl.pallas_call(lambda *refs: second_body(spans, pillars, *refs), in_specs...  2.5 us
    ppermute x1, waiting for transfers between devices, on_device(): lax.ppermute(own[1], 'bev', pairs)  1.05 us
    ppermute x3, starting transfers between devices, on_device(): lax.ppermute(own[index], 'bev', pairs)  0.68 us
  transfers between devices with their start and end apart: 10, of which 6 were waited for; matrix products, arithmetic and copies ran while one was open for 2% of the time, Pallas kernels for 0%

profile of v4, /device:TPU:0, one launch (start us, length us, event | category | flops | bytes accessed | tf_op | source)
XLA Modules:
  0.0 29.1 jit_solution(6963577066889869896)
XLA Ops:
  0.6 0.6 %collective-permute-start = (s32[1,4096]{1,0:T(1,128)}, s32[1,4096]{1,0:T(1,128)S(1)}, u32[]{:S(2)}, u32[]{:S(2)}) collective-permute-start(s32[1,4096]{1,0:T(1,128)} %bitcast.13), channel_id=1, source_target_pairs={{1,0},{0,1},{3,2},{2,3},{5,4},{4,5},{7,6},{6,7},{9,8},{8,9},{11,10... | collective-permute-start | bytes 49160 | tf_op jit(solution)/shard_map/ppermute | solution.py:394
  1.2 1.0 %collective-permute-done.refs_9_.refs_6_ = s32[1,4096]{1,0:T(1,128)S(1)} collective-permute-done((s32[1,4096]{1,0:T(1,128)}, s32[1,4096]{1,0:T(1,128)S(1)}, u32[]{:S(2)}, u32[]{:S(2)}) %collective-permute-start) | collective-permute-done | bytes 16416 | tf_op jit(solution)/shard_map/ppermute | solution.py:394
  2.2 2.8 %pool_own.1 = (f32[400,256]{1,0:T(8,128)S(1)}, bf16[64,80]{1,0:T(8,128)(2,1)S(1)}, f32[1,128]{1,0:T(1,128)S(1)}, s32[1,16]{1,0:T(1,128)S(1)}, s32[1,1536]{1,0:T(...) custom-call(s32[1,16]{1,0:T(1,128)} %bitcast.21, f32[11,11]{1,0:T(8,128)} %refs_1_.1, f32[15,64]{1,0:T(8,128)} %bitcast.19, ...), custom_call_target="tpu_custom_call" | custom-call | flops 1000000000 | bytes 1000000 | tf_op jit(solution)/shard_map/pool_own/pallas_call | solution.py:414
  5.0 3.6 %collective-permute-start.6 = (f32[1,128]{1,0:T(1,128)S(1)}, f32[1,128]{1,0:T(1,128)S(1)}, u32[]{:S(2)}, u32[]{:S(2)}) collective-permute-start(f32[1,128]{1,0:T(1,128)S(1)} %get-tuple-element.15), channel_id=1, source_target_pairs={{0,7},{1,6},{2,5},{3,4},{4,3},{5,2},{6,1},{7,0},{8,15},{9,14},{10,... | collective-permute-start | bytes 1544 | tf_op jit(solution)/shard_map/ppermute | solution.py:361
  8.6 0.5 %collective-permute-start.5 = (f32[1,128]{1,0:T(1,128)S(1)}, f32[1,128]{1,0:T(1,128)S(1)}, u32[]{:S(2)}, u32[]{:S(2)}) collective-permute-start(f32[1,128]{1,0:T(1,128)S(1)} %get-tuple-element.15), channel_id=1, source_target_pairs={{0,5},{1,4},{2,7},{3,6},{4,1},{5,0},{6,3},{7,2},{8,13},{9,12},{10,... | collective-permute-start | bytes 1544 | tf_op jit(solution)/shard_map/ppermute | solution.py:361
  9.1 0.1 collective-permute-start.4
  9.2 0.7 %collective-permute-done.6 = f32[1,128]{1,0:T(1,128)S(1)} collective-permute-done((f32[1,128]{1,0:T(1,128)S(1)}, f32[1,128]{1,0:T(1,128)S(1)}, u32[]{:S(2)}, u32[]{:S(2)}) %collective-permute-start.6) | collective-permute-done | bytes 544 | tf_op jit(solution)/shard_map/ppermute | solution.py:361
  9.9 1.7 %collective-permute-done.5 = f32[1,128]{1,0:T(1,128)S(1)} collective-permute-done((f32[1,128]{1,0:T(1,128)S(1)}, f32[1,128]{1,0:T(1,128)S(1)}, u32[]{:S(2)}, u32[]{:S(2)}) %collective-permute-start.5) | collective-permute-done | bytes 544 | tf_op jit(solution)/shard_map/ppermute | solution.py:361
  11.6 0.5 %collective-permute-done.4 = f32[1,128]{1,0:T(1,128)S(1)} collective-permute-done((f32[1,128]{1,0:T(1,128)S(1)}, f32[1,128]{1,0:T(1,128)S(1)}, u32[]{:S(2)}, u32[]{:S(2)}) %collective-permute-start.4) | collective-permute-done | bytes 544 | tf_op jit(solution)/shard_map/ppermute | solution.py:361
  12.1 3.4 %collective-permute-start.9 = (f32[1,128]{1,0:T(1,128)S(1)}, f32[1,128]{1,0:T(1,128)S(1)}, u32[]{:S(2)}, u32[]{:S(2)}) collective-permute-start(f32[1,128]{1,0:T(1,128)S(1)} %add_add_fusion), channel_id=1, source_target_pairs={{0,25},{1,24},{2,27},{3,26},{4,29},{5,28},{6,31},{7,30},{8,17},{9,... | collective-permute-start | bytes 1544 | tf_op jit(solution)/shard_map/ppermute | solution.py:361
  15.5 0.0 collective-permute-start.8
  15.5 0.6 %collective-permute-start.7 = (f32[1,128]{1,0:T(1,128)S(1)}, f32[1,128]{1,0:T(1,128)S(1)}, u32[]{:S(2)}, u32[]{:S(2)}) collective-permute-start(f32[1,128]{1,0:T(1,128)S(1)} %add_add_fusion), channel_id=1, source_target_pairs={{0,9},{1,8},{2,11},{3,10},{4,13},{5,12},{6,15},{7,14},{8,1},{9,0},... | collective-permute-start | bytes 1544 | tf_op jit(solution)/shard_map/ppermute | solution.py:361
  16.0 0.3 collective-permute-start.2
  16.3 0.2 collective-permute-start.3
  16.6 0.3 %collective-permute-done.9 = f32[1,128]{1,0:T(1,128)S(1)} collective-permute-done((f32[1,128]{1,0:T(1,128)S(1)}, f32[1,128]{1,0:T(1,128)S(1)}, u32[]{:S(2)}, u32[]{:S(2)}) %collective-permute-start.9) | collective-permute-done | bytes 544 | tf_op jit(solution)/shard_map/ppermute | solution.py:361
  16.9 0.2 collective-permute-start.1
  17.1 2.3 %collective-permute-done.8 = f32[1,128]{1,0:T(1,128)S(1)} collective-permute-done((f32[1,128]{1,0:T(1,128)S(1)}, f32[1,128]{1,0:T(1,128)S(1)}, u32[]{:S(2)}, u32[]{:S(2)}) %collective-permute-start.8) | collective-permute-done | bytes 544 | tf_op jit(solution)/shard_map/ppermute | solution.py:361
  19.4 0.0 collective-permute-done.7
  19.4 0.5 %slice_bitcast_fusion = f32[11]{0:T(128)} fusion(f32[1,128]{1,0:T(1,128)S(1)} %add_multiply_fusion), kind=kLoop, calls=%fused_computation | loop fusion | bytes 88 | tf_op jit(solution)/shard_map/squeeze | solution.py:439
  19.9 0.0 collective-permute-done.2.refs_7_
  19.9 0.0 collective-permute-done.3.refs_8_
  19.9 0.0 collective-permute-done.1.refs_5_
  19.9 2.5 %pool_rest.1.sorted_ref = f32[14,72,128]{2,1,0:T(8,128)S(1)} custom-call(s32[1,16]{1,0:T(1,128)S(1)} %get-tuple-element.10.refs_0_, bf16[64,80]{1,0:T(8,128)(2,1)S(1)} %get-tuple-element.11.refs_1_, f32[400,256]{1,0:T(8,128)S(1)} %get-tuple-element.12.refs_2_, s32[1,1536]{1,0:T(1,128)S(1)} %get-tuple-element.13.refs_3_, ...), custom_call_target="tpu_custom_call" | custom-call | flops 1000000000 | bytes 1000000 | tf_op jit(solution)/shard_map/pool_rest/pallas_call | solution.py:440
  22.4 6.8 %place.1 = bf16[64,432,248]{2,1,0:T(8,128)(2,1)} custom-call(s32[1,128]{1,0:T(1,128)S(1)} %get-tuple-element.9.starts_vmem, f32[14,72,128]{2,1,0:T(8,128)S(1)} %pool_rest.1.sorted_ref), custom_call_target="tpu_custom_call" | custom-call | flops 1000000000 | bytes 10000000 | tf_op jit(solution)/shard_map/place/pallas_call | solution.py:325
  (2 shorter events, 0.0 us)
Async XLA Ops:
  0.6 1.6 %collective-permute-start = (s32[1,4096]{1,0:T(1,128)}, s32[1,4096]{1,0:T(1,128)S(1)}, u32[]{:S(2)}, u32[]{:S(2)}) collective-permute-start(s32[1,4096]{1,0:T(1,128)} %bitcast.13), channel_id=1, source_target_pairs={{1,0},{0,1},{3,2},{2,3},{5,4},{4,5},{7,6},{6,7},{9,8},{8,9},{11,10... | collective-permute-start | bytes 49160 | tf_op jit(solution)/shard_map/ppermute | solution.py:394
  5.0 4.9 %collective-permute-start.6 = (f32[1,128]{1,0:T(1,128)S(1)}, f32[1,128]{1,0:T(1,128)S(1)}, u32[]{:S(2)}, u32[]{:S(2)}) collective-permute-start(f32[1,128]{1,0:T(1,128)S(1)} %get-tuple-element.15), channel_id=1, source_target_pairs={{0,7},{1,6},{2,5},{3,4},{4,3},{5,2},{6,1},{7,0},{8,15},{9,14},{10,... | collective-permute-start | bytes 1544 | tf_op jit(solution)/shard_map/ppermute | solution.py:361
  8.6 3.0 %collective-permute-start.5 = (f32[1,128]{1,0:T(1,128)S(1)}, f32[1,128]{1,0:T(1,128)S(1)}, u32[]{:S(2)}, u32[]{:S(2)}) collective-permute-start(f32[1,128]{1,0:T(1,128)S(1)} %get-tuple-element.15), channel_id=1, source_target_pairs={{0,5},{1,4},{2,7},{3,6},{4,1},{5,0},{6,3},{7,2},{8,13},{9,12},{10,... | collective-permute-start | bytes 1544 | tf_op jit(solution)/shard_map/ppermute | solution.py:361
  9.1 3.0 %collective-permute-start.4 = (f32[1,128]{1,0:T(1,128)S(1)}, f32[1,128]{1,0:T(1,128)S(1)}, u32[]{:S(2)}, u32[]{:S(2)}) collective-permute-start(f32[1,128]{1,0:T(1,128)S(1)} %get-tuple-element.15), channel_id=1, source_target_pairs={{0,3},{1,2},{2,1},{3,0},{4,7},{5,6},{6,5},{7,4},{8,11},{9,10},{10,... | collective-permute-start | bytes 1544 | tf_op jit(solution)/shard_map/ppermute | solution.py:361
  12.1 4.8 %collective-permute-start.9 = (f32[1,128]{1,0:T(1,128)S(1)}, f32[1,128]{1,0:T(1,128)S(1)}, u32[]{:S(2)}, u32[]{:S(2)}) collective-permute-start(f32[1,128]{1,0:T(1,128)S(1)} %add_add_fusion), channel_id=1, source_target_pairs={{0,25},{1,24},{2,27},{3,26},{4,29},{5,28},{6,31},{7,30},{8,17},{9,... | collective-permute-start | bytes 1544 | tf_op jit(solution)/shard_map/ppermute | solution.py:361
  15.5 3.9 %collective-permute-start.8 = (f32[1,128]{1,0:T(1,128)S(1)}, f32[1,128]{1,0:T(1,128)S(1)}, u32[]{:S(2)}, u32[]{:S(2)}) collective-permute-start(f32[1,128]{1,0:T(1,128)S(1)} %add_add_fusion), channel_id=1, source_target_pairs={{0,17},{1,16},{2,19},{3,18},{4,21},{5,20},{6,23},{7,22},{8,25},{9,... | collective-permute-start | bytes 1544 | tf_op jit(solution)/shard_map/ppermute | solution.py:361
  15.5 3.9 %collective-permute-start.7 = (f32[1,128]{1,0:T(1,128)S(1)}, f32[1,128]{1,0:T(1,128)S(1)}, u32[]{:S(2)}, u32[]{:S(2)}) collective-permute-start(f32[1,128]{1,0:T(1,128)S(1)} %add_add_fusion), channel_id=1, source_target_pairs={{0,9},{1,8},{2,11},{3,10},{4,13},{5,12},{6,15},{7,14},{8,1},{9,0},... | collective-permute-start | bytes 1544 | tf_op jit(solution)/shard_map/ppermute | solution.py:361
  16.0 3.8 %collective-permute-start.2 = (s32[1,4096]{1,0:T(1,128)}, s32[1,4096]{1,0:T(1,128)S(1)}, u32[]{:S(2)}, u32[]{:S(2)}) collective-permute-start(s32[1,4096]{1,0:T(1,128)} %bitcast.16), channel_id=1, source_target_pairs={{1,0},{0,1},{3,2},{2,3},{5,4},{4,5},{7,6},{6,7},{9,8},{8,9},{11,10... | collective-permute-start | bytes 49160 | tf_op jit(solution)/shard_map/ppermute | solution.py:398
  16.3 3.6 %collective-permute-start.3 = (s32[1,4096]{1,0:T(1,128)}, s32[1,4096]{1,0:T(1,128)S(1)}, u32[]{:S(2)}, u32[]{:S(2)}) collective-permute-start(s32[1,4096]{1,0:T(1,128)} %bitcast.18), channel_id=1, source_target_pairs={{1,0},{0,1},{3,2},{2,3},{5,4},{4,5},{7,6},{6,7},{9,8},{8,9},{11,10... | collective-permute-start | bytes 49160 | tf_op jit(solution)/shard_map/ppermute | solution.py:398
  16.9 3.0 %collective-permute-start.1 = (f32[4,4096]{1,0:T(4,128)}, f32[4,4096]{1,0:T(4,128)S(1)}, u32[]{:S(2)}, u32[]{:S(2)}) collective-permute-start(f32[4,4096]{1,0:T(4,128)} %refs_5_.1), channel_id=1, source_target_pairs={{1,0},{0,1},{3,2},{2,3},{5,4},{4,5},{7,6},{6,7},{9,8},{8,9},{11,10... | collective-permute-start | bytes 196616 | tf_op jit(solution)/shard_map/ppermute | solution.py:398

commit v5 on v4

--- a/solution.py
+++ b/solution.py
@@ -193,9 +193,13 @@
     order_pillars(pillars, sub_of, cell_ref, cell_pad, rank_ref, where_ref, starts_ref)
 
 
-def second_body(spans, pillars, counts_ref, matrix_ref, sums_in_ref, rank_ref, where_ref, *refs):
+def second_body(
+    spans, pillars, counts_ref, matrix_ref, sums_in_ref, rank_ref, where_ref, starts_ref, *refs
+):
     parts = len(spans)
-    (sorted_ref,) = refs[4 * parts :]
+    sorted_ref, starts_smem, sem = refs[4 * parts :]
+    move = pltpu.make_async_copy(starts_ref, starts_smem, sem)
+    move.start()
     channels = matrix_ref.shape[0]
     hi_count = round_up(pillars, LO) // LO
     sums = sums_in_ref[...]
@@ -229,14 +233,12 @@
     for chunk in range(2 * hi_count, 2 * hi_count + 2):
         sorted_ref[chunk, :channels, :] = jnp.zeros((channels, 128), jnp.float32)
         sorted_ref[chunk, channels:, :] = jnp.full((8, 128), -1.0, jnp.float32)
-
-
-def place_body(starts_vmem, sorted_ref, out_ref, starts_ref, image, lane_hot, acc_ref, sem, sems):
-    fetch = pltpu.make_async_copy(starts_vmem, starts_ref, sem)
-    fetch.start()
-    fetch.wait()
+    move.wait()
+
+
+def place_body(starts_ref, sorted_ref, out_ref, image, acc_ref, sems):
     channels, _, lanes = out_ref.shape
-    chunks, wide, _ = lane_hot.shape
+    wide = acc_ref.shape[1]
     blocks = image.shape[1] // STEP
 
     def hot_of(chunk):
@@ -246,7 +248,7 @@
     def base_of(block):
         return starts_ref[0, block] >> 7
 
-    def partial(block, turn, ready=True):
+    def partial(block, turn):
         talls = []
         hots = []
         for half in range(2):
@@ -261,7 +263,7 @@
                     jnp.concatenate([row * mask_a, row * mask_b], axis=0).astype(jnp.bfloat16)
                 )
             talls.append(jnp.concatenate(tall, axis=0))
-            hots.append(lane_hot[chunk] if ready else hot_of(chunk))
+            hots.append(hot_of(chunk))
         return lax.dot_general(
             jnp.concatenate(talls, axis=1),
             jnp.concatenate(hots, axis=1),
@@ -277,7 +279,7 @@
     spans = []
     begin = 0
     while begin < blocks:
-        end = min(begin + min(len(spans) + 1, GROUP), blocks)
+        end = min(begin + min(len(spans) // 2 + 1, GROUP), blocks)
         spans.append((begin, end))
         begin = end
     copies = []
@@ -290,11 +292,7 @@
 
     @pl.when(spread == 0)
     def _():
-        put(0, partial(0, 0, ready=False))
-        copies[0].start()
-        for chunk in range(chunks):
-            lane_hot[chunk] = hot_of(chunk)
-        for (begin, end), copy in zip(spans[1:], copies[1:]):
+        for (begin, end), copy in zip(spans, copies):
             for block in range(begin, end):
                 put(block, partial(block, 0))
             copy.start()
@@ -304,11 +302,11 @@
         @pl.loop(0, blocks)
         def _(block):
             turns = (starts_ref[0, block + 1] - base_of(block) * 128 + LO - 1) // LO
-            acc_ref[...] = partial(block, 0, ready=False)
+            acc_ref[...] = partial(block, 0)
 
             @pl.loop(1, turns)
             def _(turn):
-                acc_ref[...] += partial(block, turn, ready=False)
+                acc_ref[...] += partial(block, turn)
 
             put(pl.multiple_of(block, 1), acc_ref[...])
 
@@ -325,22 +323,19 @@
     return pl.pallas_call(
         place_body,
         in_specs=[
-            pl.BlockSpec(memory_space=pltpu.VMEM),
+            pl.BlockSpec(memory_space=pltpu.SMEM),
             pl.BlockSpec(memory_space=pltpu.VMEM),
         ],
         out_specs=pl.BlockSpec(memory_space=pl.ANY),
         scratch_shapes=[
-            pltpu.SMEM((1, 128), jnp.int32),
             pltpu.VMEM((channels, blocks * STEP, lanes), jnp.bfloat16),
-            pltpu.VMEM((sorted_values.shape[0], wide, 128), jnp.bfloat16),
             pltpu.VMEM((channels * STEP, wide), jnp.float32),
-            pltpu.SemaphoreType.DMA,
             pltpu.SemaphoreType.DMA((blocks,)),
         ],
         out_shape=jax.ShapeDtypeStruct((channels, blocks * STEP, lanes), jnp.bfloat16),
         cost_estimate=pl.CostEstimate(flops=10**9, transcendentals=0, bytes_accessed=10**7),
         name="place",
-    )(in_vmem(starts), in_vmem(sorted_values))[:, :subs]
+    )(pltpu.with_memory_space_constraint(starts, pltpu.SMEM), in_vmem(sorted_values))[:, :subs]
 
 
 def in_vmem(value):
@@ -437,14 +432,18 @@
         *other_classes,
     )
     class_counts = (all_tallies(tally, frames, band_count) / total)[0, :CLASSES]
-    sorted_values = pl.pallas_call(
+    sorted_values, starts = pl.pallas_call(
         lambda *refs: second_body(spans, pillars, *refs),
-        in_specs=[vmem] * (5 + len(others)),
-        out_specs=vmem,
-        out_shape=pltpu.VMEM(((width + LO) // 128, channels + 8, 128), jnp.float32),
+        in_specs=[vmem] * (6 + len(others)),
+        out_specs=(vmem, pl.BlockSpec(memory_space=pltpu.SMEM)),
+        out_shape=(
+            pltpu.VMEM(((width + LO) // 128, channels + 8, 128), jnp.float32),
+            pltpu.SMEM((1, 128), jnp.int32),
+        ),
+        scratch_shapes=[pltpu.SemaphoreType.DMA],
         cost_estimate=pl.CostEstimate(flops=10**9, transcendentals=0, bytes_accessed=10**6),
         name="pool_rest",
-    )(*[in_vmem(x) for x in (counts, matrix, sums, rank, where)], *others)
+    )(*[in_vmem(x) for x in (counts, matrix, sums, rank, where, starts)], *others)
     planes = place(sorted_values, starts, channels, subs, lanes)
     bev_image = planes.swapaxes(1, 2) if sub_of == "col" else planes
     return (bev_image[None], class_counts)

time: 29.3 us -> 28.5 us (0.973)
  Pallas kernels: 12 us -> 11.2 us
    pallas_call x1, Pallas kernels: 6.76 us -> 5.92 us  [place(): pl.pallas_call(place_body, in_specs=[pl.BlockSpec(memory_space=pltpu.SMEM...]
where the time goes in v5:
time: 28.5 us; the launch traced here: 28.3 us
  Pallas kernels  11.2 us (39%)
  starting transfers between devices  9.4 us (33%)
  waiting for transfers between devices  6.54 us (23%)
  between operations  0.66 us (2%)
  local copies, waits for them, and re-layouts  0.51 us (2%)
    ppermute x6, starting transfers between devices, all_tallies(): received.append(lax.ppermute(total, ('pts', 'bev'), pairs))  8.16 us
    pallas_call x1, Pallas kernels, place(): pl.pallas_call(place_body, in_specs=[pl.BlockSpec(memory_space=pltpu.SMEM...  5.92 us
    ppermute x6, waiting for transfers between devices, all_tallies(): received.append(lax.ppermute(total, ('pts', 'bev'), pairs))  5.48 us
    pallas_call x1, Pallas kernels, on_device(): pl.pallas_call(lambda *refs: first_body(own_span, spans, pillars, sub_of,...  2.77 us
    pallas_call x1, Pallas kernels, on_device(): pl.pallas_call(lambda *refs: second_body(spans, pillars, *refs), in_specs...  2.52 us
    ppermute x1, waiting for transfers between devices, on_device(): lax.ppermute(own[1], 'bev', pairs)  1.05 us
    ppermute x3, starting transfers between devices, on_device(): lax.ppermute(own[index], 'bev', pairs)  0.69 us
  transfers between devices with their start and end apart: 10, of which 6 were waited for; matrix products, arithmetic and copies ran while one was open for 2% of the time, Pallas kernels for 0%

profile of v5, /device:TPU:0, one launch (start us, length us, event | category | flops | bytes accessed | tf_op | source)
XLA Modules:
  0.0 28.3 jit_solution(6499092923532759894)
XLA Ops:
  0.6 0.6 %collective-permute-start = (s32[1,4096]{1,0:T(1,128)}, s32[1,4096]{1,0:T(1,128)S(1)}, u32[]{:S(2)}, u32[]{:S(2)}) collective-permute-start(s32[1,4096]{1,0:T(1,128)} %bitcast.13), channel_id=1, source_target_pairs={{1,0},{0,1},{3,2},{2,3},{5,4},{4,5},{7,6},{6,7},{9,8},{8,9},{11,10... | collective-permute-start | bytes 49160 | tf_op jit(solution)/shard_map/ppermute | solution.py:389
  1.2 1.0 %collective-permute-done.refs_9_.refs_7_ = s32[1,4096]{1,0:T(1,128)S(1)} collective-permute-done((s32[1,4096]{1,0:T(1,128)}, s32[1,4096]{1,0:T(1,128)S(1)}, u32[]{:S(2)}, u32[]{:S(2)}) %collective-permute-start) | collective-permute-done | bytes 16416 | tf_op jit(solution)/shard_map/ppermute | solution.py:389
  2.2 2.8 %pool_own.1 = (f32[400,256]{1,0:T(8,128)S(1)}, bf16[64,80]{1,0:T(8,128)(2,1)S(1)}, f32[1,128]{1,0:T(1,128)S(1)}, s32[1,16]{1,0:T(1,128)S(1)}, s32[1,1536]{1,0:T(...) custom-call(s32[1,16]{1,0:T(1,128)} %bitcast.21, f32[11,11]{1,0:T(8,128)} %refs_1_.1, f32[15,64]{1,0:T(8,128)} %bitcast.19, ...), custom_call_target="tpu_custom_call" | custom-call | flops 1000000000 | bytes 1000000 | tf_op jit(solution)/shard_map/pool_own/pallas_call | solution.py:409
  5.0 3.6 %collective-permute-start.6 = (f32[1,128]{1,0:T(1,128)S(1)}, f32[1,128]{1,0:T(1,128)S(1)}, u32[]{:S(2)}, u32[]{:S(2)}) collective-permute-start(f32[1,128]{1,0:T(1,128)S(1)} %get-tuple-element.19), channel_id=1, source_target_pairs={{0,7},{1,6},{2,5},{3,4},{4,3},{5,2},{6,1},{7,0},{8,15},{9,14},{10,... | collective-permute-start | bytes 1544 | tf_op jit(solution)/shard_map/ppermute | solution.py:356
  8.6 0.5 %collective-permute-start.5 = (f32[1,128]{1,0:T(1,128)S(1)}, f32[1,128]{1,0:T(1,128)S(1)}, u32[]{:S(2)}, u32[]{:S(2)}) collective-permute-start(f32[1,128]{1,0:T(1,128)S(1)} %get-tuple-element.19), channel_id=1, source_target_pairs={{0,5},{1,4},{2,7},{3,6},{4,1},{5,0},{6,3},{7,2},{8,13},{9,12},{10,... | collective-permute-start | bytes 1544 | tf_op jit(solution)/shard_map/ppermute | solution.py:356
  9.1 0.1 collective-permute-start.4
  9.2 0.7 %collective-permute-done.6 = f32[1,128]{1,0:T(1,128)S(1)} collective-permute-done((f32[1,128]{1,0:T(1,128)S(1)}, f32[1,128]{1,0:T(1,128)S(1)}, u32[]{:S(2)}, u32[]{:S(2)}) %collective-permute-start.6) | collective-permute-done | bytes 544 | tf_op jit(solution)/shard_map/ppermute | solution.py:356
  9.9 1.7 %collective-permute-done.5 = f32[1,128]{1,0:T(1,128)S(1)} collective-permute-done((f32[1,128]{1,0:T(1,128)S(1)}, f32[1,128]{1,0:T(1,128)S(1)}, u32[]{:S(2)}, u32[]{:S(2)}) %collective-permute-start.5) | collective-permute-done | bytes 544 | tf_op jit(solution)/shard_map/ppermute | solution.py:356
  11.6 0.5 %collective-permute-done.4 = f32[1,128]{1,0:T(1,128)S(1)} collective-permute-done((f32[1,128]{1,0:T(1,128)S(1)}, f32[1,128]{1,0:T(1,128)S(1)}, u32[]{:S(2)}, u32[]{:S(2)}) %collective-permute-start.4) | collective-permute-done | bytes 544 | tf_op jit(solution)/shard_map/ppermute | solution.py:356
  12.1 3.4 %collective-permute-start.9 = (f32[1,128]{1,0:T(1,128)S(1)}, f32[1,128]{1,0:T(1,128)S(1)}, u32[]{:S(2)}, u32[]{:S(2)}) collective-permute-start(f32[1,128]{1,0:T(1,128)S(1)} %add_add_fusion), channel_id=1, source_target_pairs={{0,25},{1,24},{2,27},{3,26},{4,29},{5,28},{6,31},{7,30},{8,17},{9,... | collective-permute-start | bytes 1544 | tf_op jit(solution)/shard_map/ppermute | solution.py:356
  15.5 0.0 collective-permute-start.8
  15.5 0.6 %collective-permute-start.7 = (f32[1,128]{1,0:T(1,128)S(1)}, f32[1,128]{1,0:T(1,128)S(1)}, u32[]{:S(2)}, u32[]{:S(2)}) collective-permute-start(f32[1,128]{1,0:T(1,128)S(1)} %add_add_fusion), channel_id=1, source_target_pairs={{0,9},{1,8},{2,11},{3,10},{4,13},{5,12},{6,15},{7,14},{8,1},{9,0},... | collective-permute-start | bytes 1544 | tf_op jit(solution)/shard_map/ppermute | solution.py:356
  16.0 0.3 collective-permute-start.2
  16.3 0.2 collective-permute-start.3
  16.6 0.3 %collective-permute-done.9 = f32[1,128]{1,0:T(1,128)S(1)} collective-permute-done((f32[1,128]{1,0:T(1,128)S(1)}, f32[1,128]{1,0:T(1,128)S(1)}, u32[]{:S(2)}, u32[]{:S(2)}) %collective-permute-start.9) | collective-permute-done | bytes 544 | tf_op jit(solution)/shard_map/ppermute | solution.py:356
  16.9 0.2 collective-permute-start.1
  17.1 2.3 %collective-permute-done.8 = f32[1,128]{1,0:T(1,128)S(1)} collective-permute-done((f32[1,128]{1,0:T(1,128)S(1)}, f32[1,128]{1,0:T(1,128)S(1)}, u32[]{:S(2)}, u32[]{:S(2)}) %collective-permute-start.8) | collective-permute-done | bytes 544 | tf_op jit(solution)/shard_map/ppermute | solution.py:356
  19.4 0.0 collective-permute-done.7
  19.4 0.5 %slice_bitcast_fusion = f32[11]{0:T(128)} fusion(f32[1,128]{1,0:T(1,128)S(1)} %add_multiply_fusion), kind=kLoop, calls=%fused_computation | loop fusion | bytes 88 | tf_op jit(solution)/shard_map/squeeze | solution.py:434
  19.9 0.0 collective-permute-done.2.refs_8_
  19.9 0.0 collective-permute-done.3.refs_9_
  19.9 0.0 collective-permute-done.1.refs_6_
  19.9 2.5 %pool_rest.1 = (f32[14,72,128]{2,1,0:T(8,128)S(1)}, s32[1,128]{1,0:T(1,128)S(4)}) custom-call(s32[1,16]{1,0:T(1,128)S(1)} %get-tuple-element.11.refs_0_, bf16[64,80]{1,0:T(8,128)(2,1)S(1)} %get-tuple-element.12.refs_1_, f32[400,256]{1,0:T(8,128)S(1)} %get-tuple-element.13.refs_2_, s32[1,1536]{1,0:T(1,128)S(1)} %get-tuple-element.14.refs_3_, ...), custom_call_target="tpu_custom_call" | custom-call | flops 1000000000 | bytes 1000000 | tf_op jit(solution)/shard_map/pool_rest/pallas_call | solution.py:435
  22.4 5.9 %place.1 = bf16[64,432,248]{2,1,0:T(8,128)(2,1)} custom-call(s32[1,128]{1,0:T(1,128)S(4)} %get-tuple-element.17.starts_ref, f32[14,72,128]{2,1,0:T(8,128)S(1)} %get-tuple-element.18.sorted_ref), custom_call_target="tpu_custom_call" | custom-call | flops 1000000000 | bytes 10000000 | tf_op jit(solution)/shard_map/place/pallas_call | solution.py:323
  (2 shorter events, 0.0 us)
Async XLA Ops:
  0.6 1.6 %collective-permute-start = (s32[1,4096]{1,0:T(1,128)}, s32[1,4096]{1,0:T(1,128)S(1)}, u32[]{:S(2)}, u32[]{:S(2)}) collective-permute-start(s32[1,4096]{1,0:T(1,128)} %bitcast.13), channel_id=1, source_target_pairs={{1,0},{0,1},{3,2},{2,3},{5,4},{4,5},{7,6},{6,7},{9,8},{8,9},{11,10... | collective-permute-start | bytes 49160 | tf_op jit(solution)/shard_map/ppermute | solution.py:389
  5.0 4.9 %collective-permute-start.6 = (f32[1,128]{1,0:T(1,128)S(1)}, f32[1,128]{1,0:T(1,128)S(1)}, u32[]{:S(2)}, u32[]{:S(2)}) collective-permute-start(f32[1,128]{1,0:T(1,128)S(1)} %get-tuple-element.19), channel_id=1, source_target_pairs={{0,7},{1,6},{2,5},{3,4},{4,3},{5,2},{6,1},{7,0},{8,15},{9,14},{10,... | collective-permute-start | bytes 1544 | tf_op jit(solution)/shard_map/ppermute | solution.py:356
  8.6 3.0 %collective-permute-start.5 = (f32[1,128]{1,0:T(1,128)S(1)}, f32[1,128]{1,0:T(1,128)S(1)}, u32[]{:S(2)}, u32[]{:S(2)}) collective-permute-start(f32[1,128]{1,0:T(1,128)S(1)} %get-tuple-element.19), channel_id=1, source_target_pairs={{0,5},{1,4},{2,7},{3,6},{4,1},{5,0},{6,3},{7,2},{8,13},{9,12},{10,... | collective-permute-start | bytes 1544 | tf_op jit(solution)/shard_map/ppermute | solution.py:356
  9.1 3.0 %collective-permute-start.4 = (f32[1,128]{1,0:T(1,128)S(1)}, f32[1,128]{1,0:T(1,128)S(1)}, u32[]{:S(2)}, u32[]{:S(2)}) collective-permute-start(f32[1,128]{1,0:T(1,128)S(1)} %get-tuple-element.19), channel_id=1, source_target_pairs={{0,3},{1,2},{2,1},{3,0},{4,7},{5,6},{6,5},{7,4},{8,11},{9,10},{10,... | collective-permute-start | bytes 1544 | tf_op jit(solution)/shard_map/ppermute | solution.py:356
  12.1 4.8 %collective-permute-start.9 = (f32[1,128]{1,0:T(1,128)S(1)}, f32[1,128]{1,0:T(1,128)S(1)}, u32[]{:S(2)}, u32[]{:S(2)}) collective-permute-start(f32[1,128]{1,0:T(1,128)S(1)} %add_add_fusion), channel_id=1, source_target_pairs={{0,25},{1,24},{2,27},{3,26},{4,29},{5,28},{6,31},{7,30},{8,17},{9,... | collective-permute-start | bytes 1544 | tf_op jit(solution)/shard_map/ppermute | solution.py:356
  15.5 3.9 %collective-permute-start.8 = (f32[1,128]{1,0:T(1,128)S(1)}, f32[1,128]{1,0:T(1,128)S(1)}, u32[]{:S(2)}, u32[]{:S(2)}) collective-permute-start(f32[1,128]{1,0:T(1,128)S(1)} %add_add_fusion), channel_id=1, source_target_pairs={{0,17},{1,16},{2,19},{3,18},{4,21},{5,20},{6,23},{7,22},{8,25},{9,... | collective-permute-start | bytes 1544 | tf_op jit(solution)/shard_map/ppermute | solution.py:356
  15.5 3.9 %collective-permute-start.7 = (f32[1,128]{1,0:T(1,128)S(1)}, f32[1,128]{1,0:T(1,128)S(1)}, u32[]{:S(2)}, u32[]{:S(2)}) collective-permute-start(f32[1,128]{1,0:T(1,128)S(1)} %add_add_fusion), channel_id=1, source_target_pairs={{0,9},{1,8},{2,11},{3,10},{4,13},{5,12},{6,15},{7,14},{8,1},{9,0},... | collective-permute-start | bytes 1544 | tf_op jit(solution)/shard_map/ppermute | solution.py:356
  16.0 3.8 %collective-permute-start.2 = (s32[1,4096]{1,0:T(1,128)}, s32[1,4096]{1,0:T(1,128)S(1)}, u32[]{:S(2)}, u32[]{:S(2)}) collective-permute-start(s32[1,4096]{1,0:T(1,128)} %bitcast.16), channel_id=1, source_target_pairs={{1,0},{0,1},{3,2},{2,3},{5,4},{4,5},{7,6},{6,7},{9,8},{8,9},{11,10... | collective-permute-start | bytes 49160 | tf_op jit(solution)/shard_map/ppermute | solution.py:393
  16.3 3.6 %collective-permute-start.3 = (s32[1,4096]{1,0:T(1,128)}, s32[1,4096]{1,0:T(1,128)S(1)}, u32[]{:S(2)}, u32[]{:S(2)}) collective-permute-start(s32[1,4096]{1,0:T(1,128)} %bitcast.18), channel_id=1, source_target_pairs={{1,0},{0,1},{3,2},{2,3},{5,4},{4,5},{7,6},{6,7},{9,8},{8,9},{11,10... | collective-permute-start | bytes 49160 | tf_op jit(solution)/shard_map/ppermute | solution.py:393
  16.9 3.0 %collective-permute-start.1 = (f32[4,4096]{1,0:T(4,128)}, f32[4,4096]{1,0:T(4,128)S(1)}, u32[]{:S(2)}, u32[]{:S(2)}) collective-permute-start(f32[4,4096]{1,0:T(4,128)} %refs_5_.1), channel_id=1, source_target_pairs={{1,0},{0,1},{3,2},{2,3},{5,4},{4,5},{7,6},{6,7},{9,8},{8,9},{11,10... | collective-permute-start | bytes 196616 | tf_op jit(solution)/shard_map/ppermute | solution.py:393
